TPU v7x, 8 devices: a whole 2x2x1 slice. The times are simulated.
8 devices in a mesh: col: 2 (over z, y), row: 4 (over x, core).
Axes of the slice: x: 2, y: 2, z: 1, core: 2. Of those that a mesh axis runs over, the one named last changes fastest.
Arguments:
- x_in: bfloat16 [16384, 2048], P('row', 'col')
- ln_gain: float32 [2048], P('col')
- ln_bias: float32 [2048], P('col')
- w_up: bfloat16 [2048, 8192], P('row', 'col')
- b_up: bfloat16 [8192], P('col')
- w_down: bfloat16 [8192, 2048], P('row', 'col')
- b_down: bfloat16 [2048], P('col')
- dy_out: bfloat16 [16384, 2048], P('row', 'col')
Outputs:
- output 1: bfloat16 [16384, 2048], P('row', 'col')
- output 2: bfloat16 [16384, 2048], P('row', 'col')
- output 3: bfloat16 [2048, 8192], P('row', 'col')
- output 4: float32 [8192], P('col')
- output 5: bfloat16 [8192, 2048], P('row', 'col')
- output 6: float32 [2048], P('col')
- output 7: float32 [2048], P('col')
- output 8: float32 [2048], P('col')
All inputs are finite; a program needn't handle non-finite values.
Results may differ from a plain program's by a relative error of at most 0.0112855.
Values are sent between devices in bfloat16 or wider.
A program may use at most 1 GiB of HBM per device.

v0:
```python
import jax
import jax.numpy as jnp
from jax import lax
from jax.sharding import PartitionSpec as P

LN_EPS = 1e-5
GELU_K = 0.7978845608028654
GELU_A = 0.044715
CONTRACT_ROWS = (((0,), (0,)), ((), ()))
CONTRACT_COLS = (((1,), (1,)), ((), ()))


def gelu_grad(u_val):
    tanh_val = jnp.tanh(GELU_K * (u_val + GELU_A * u_val * u_val * u_val))
    slope = GELU_K * (1.0 + 3.0 * GELU_A * u_val * u_val)
    return 0.5 * (1.0 + tanh_val) + 0.5 * u_val * (1.0 - tanh_val * tanh_val) * slope


def solution(mesh):
    def local_step(x_in, ln_gain, ln_bias, w_up, b_up, w_down, b_down, dy_out):
        width = x_in.shape[1] * mesh.shape['col']
        x_f32 = x_in.astype(jnp.float32)
        stats = jnp.concatenate([jnp.sum(x_f32, axis=1, keepdims=True), jnp.sum(x_f32 * x_f32, axis=1, keepdims=True)], axis=1)
        stats = lax.psum(stats, 'col')
        mean_x = stats[:, 0:1] / width
        mean_sq = stats[:, 1:2] / width
        inv_std = lax.rsqrt(mean_sq - mean_x * mean_x + LN_EPS)
        x_hat = (x_f32 - mean_x) * inv_std
        z_act = (x_hat * ln_gain + ln_bias).astype(jnp.bfloat16)
        z_rows = lax.all_gather(z_act, 'col', axis=1, tiled=True)
        w_up_cols = lax.all_gather(w_up, 'row', axis=0, tiled=True)
        u_pre = (jnp.dot(z_rows, w_up_cols, preferred_element_type=jnp.float32) + b_up.astype(jnp.float32)).astype(jnp.bfloat16)
        u_f32 = u_pre.astype(jnp.float32)
        a_act = jax.nn.gelu(u_f32, approximate=True).astype(jnp.bfloat16)
        a_rows = lax.all_gather(a_act, 'col', axis=1, tiled=True)
        w_down_cols = lax.all_gather(w_down, 'row', axis=0, tiled=True)
        y_out = (x_f32 + jnp.dot(a_rows, w_down_cols, preferred_element_type=jnp.float32) + b_down.astype(jnp.float32)).astype(jnp.bfloat16)
        dy_f32 = dy_out.astype(jnp.float32)
        da_part = lax.dot_general(dy_out, w_down_cols, CONTRACT_COLS, preferred_element_type=jnp.float32)
        d_act = lax.psum_scatter(da_part, 'col', scatter_dimension=1, tiled=True)
        du_pre = (d_act * gelu_grad(u_f32)).astype(jnp.bfloat16)
        dwd_part = lax.dot_general(a_rows, dy_out, CONTRACT_ROWS, preferred_element_type=jnp.float32)
        dw_down = lax.psum_scatter(dwd_part, 'row', scatter_dimension=0, tiled=True).astype(jnp.bfloat16)
        db_down = lax.psum(jnp.sum(dy_f32, axis=0), 'row')
        dwu_part = lax.dot_general(z_rows, du_pre, CONTRACT_ROWS, preferred_element_type=jnp.float32)
        dw_up = lax.psum_scatter(dwu_part, 'row', scatter_dimension=0, tiled=True).astype(jnp.bfloat16)
        db_up = lax.psum(jnp.sum(du_pre.astype(jnp.float32), axis=0), 'row')
        dz_part = lax.dot_general(du_pre, w_up_cols, CONTRACT_COLS, preferred_element_type=jnp.float32)
        dz_act = lax.psum_scatter(dz_part, 'col', scatter_dimension=1, tiled=True)
        ln_sums = lax.psum(jnp.stack([jnp.sum(dz_act * x_hat, axis=0), jnp.sum(dz_act, axis=0)]), 'row')
        value_a6 = dz_act * ln_gain
        row_sums = jnp.concatenate([jnp.sum(value_a6, axis=1, keepdims=True), jnp.sum(value_a6 * x_hat, axis=1, keepdims=True)], axis=1)
        row_sums = lax.psum(row_sums, 'col')
        mean_dxh = row_sums[:, 0:1] / width
        mean_dxh_xh = row_sums[:, 1:2] / width
        dx_in = (dy_f32 + inv_std * (value_a6 - mean_dxh - x_hat * mean_dxh_xh)).astype(jnp.bfloat16)
        return (y_out, dx_in, dw_up, db_up, dw_down, db_down, ln_sums[0], ln_sums[1])

    blk_spec = P('row', 'col')
    vec_spec = P('col')
    return jax.shard_map(local_step, mesh=mesh, in_specs=(blk_spec, vec_spec, vec_spec, blk_spec, vec_spec, blk_spec, vec_spec, blk_spec), out_specs=(blk_spec, blk_spec, blk_spec, vec_spec, blk_spec, vec_spec, vec_spec, vec_spec), check_vma=False)
```

profile of v0, /device:TPU:0, one launch (start us, length us, event | category | flops | bytes accessed | tf_op | source)
XLA Modules:
  0.0 3608.6 jit_solution(12884117285629160383)
XLA Ops:
  7.2 0.0 all-gather.11.cloned.1.call-start
  7.2 0.7 all-gather.11.cloned.1.call-update
  7.9 0.0 all-gather.5.cloned.1.call-start
  7.9 5.8 convert_reduce_fusion.1
  13.8 10.3 psum.35
  24.2 0.0 copy-start
  24.2 0.0 copy-start.2
  24.2 0.6 copy-done
  24.8 0.0 copy-done.2
  24.8 8.5 fusion.23
  33.3 0.0 all-gather.5.cloned.1.call-update
  33.3 0.0 all-gather.7.cloned.1.call-start
  33.4 0.7 all-gather.7.cloned.1.call-update
  34.0 0.3 reduce-scatter.5.cloned.1.call-start
  34.3 82.2 %all-gather.11.cloned.1.call-done = bf16[8192,1024]{1,0:T(8,128)(2,1)} async-done(((bf16[2048,1024]{1,0:T(8,128)(2,1)}), bf16[8192,1024]{1,0:T(8,128)(2,1)}) %all-gather.11.cloned.1.call-update) | async-done | bytes 16777232 | tf_op jit(solution)/shard_map/all_gather | solution.py:36
  116.5 81.3 %fusion.33 = f32[4096,8192]{1,0:T(8,128)} fusion(bf16[4096,1024]{1,0:T(8,128)(2,1)} %param.15, bf16[8192,1024]{1,0:T(8,128)(2,1)} %all-gather.11.cloned.1.call-done), kind=kOutput, calls=%fused_computation.60 | convolution fusion | flops 68719476736 | bytes 159383552 | tf_op jit(solution)/shard_map/dot_general | solution.py:39
  197.9 0.0 copy-start.6
  197.9 0.0 reduce-scatter.5.cloned.1.call-update
  197.9 0.4 all-gather.9.cloned.1.call-start
  198.3 0.3 copy-done.6
  198.6 116.8 %all-gather.5.cloned.1.call-done = bf16[4096,2048]{1,0:T(8,128)(2,1)} async-done(((bf16[4096,1024]{1,0:T(8,128)(2,1)}), bf16[4096,2048]{1,0:T(8,128)(2,1)}) %all-gather.5.cloned.1.call-update) | async-done | bytes 16777232 | tf_op jit(solution)/shard_map/all_gather | solution.py:30
  315.4 105.7 %all-gather.7.cloned.1.call-done = bf16[2048,4096]{1,0:T(8,128)(2,1)} async-done(((bf16[512,4096]{1,0:T(8,128)(2,1)}), bf16[2048,4096]{1,0:T(8,128)(2,1)}) %all-gather.7.cloned.1.call-update) | async-done | bytes 16777232 | tf_op jit(solution)/shard_map/all_gather | solution.py:31
  421.1 1446.8 %reduce-scatter.5.cloned.1.call-done = f32[4096,4096]{1,0:T(8,128)} async-done(((f32[4096,8192]{1,0:T(8,128)}), f32[4096,4096]{1,0:T(8,128)}) %reduce-scatter.5.cloned.1.call-update) | async-done | bytes 67108880 | tf_op jit(solution)/shard_map/reduce_scatter | solution.py:40
  1868.0 138.6 %convert_reduce_fusion = (f32[4096]{0:T(1024)}, bf16[4096,4096]{1,0:T(8,128)(2,1)}, bf16[4096,4096]{1,0:T(8,128)(2,1)}) fusion(f32[4096,4096]{1,0:T(8,128)} %reduce-scatter.5.cloned.1.call-done, f32[4096]{0:T(1024)S(1)} %convert_element_type.44, bf16[4096,2048]{1,0:T(8,128)(2,1)} %all-gather.5.cloned.1.call-done, ...), kind=kOutput, calls=%fused_computation.26 | convolution fusion | flops 69273124864 | bytes 167804928 | tf_op jit(solution)/shard_map/dot_general | solution.py:32
  2006.5 0.0 all-gather.9.cloned.1.call-update
  2006.5 10.7 reduce-scatter.9.cloned.1.call-start
  2017.3 79.4 %fusion.35 = f32[2048,4096]{1,0:T(8,128)} fusion(bf16[4096,2048]{1,0:T(8,128)(2,1)} %all-gather.5.cloned.1.call-done, bf16[4096,4096]{1,0:T(8,128)(2,1)} %get-tuple-element.18), kind=kOutput, calls=%fused_computation.62 | convolution fusion | flops 68719476736 | bytes 83886080 | tf_op jit(solution)/shard_map/dot_general | solution.py:45
  2096.6 0.0 reduce-scatter.9.cloned.1.call-update
  2096.7 0.0 reduce-scatter.7.cloned.1.call-start
  2096.7 78.6 %fusion.34 = f32[4096,2048]{1,0:T(8,128)} fusion(bf16[4096,4096]{1,0:T(8,128)(2,1)} %get-tuple-element.18, bf16[2048,4096]{1,0:T(8,128)(2,1)} %all-gather.7.cloned.1.call-done), kind=kOutput, calls=%fused_computation.61 | convolution fusion | flops 68719476736 | bytes 83886080 | tf_op jit(solution)/shard_map/dot_general | solution.py:48
  2175.3 0.0 reduce-scatter.7.cloned.1.call-update
  2175.3 0.3 reduce-scatter.11.cloned.1.call-start
  2175.6 594.3 %all-gather.9.cloned.1.call-done = bf16[4096,8192]{1,0:T(8,128)(2,1)} async-done(((bf16[4096,4096]{1,0:T(8,128)(2,1)}), bf16[4096,8192]{1,0:T(8,128)(2,1)}) %all-gather.9.cloned.1.call-update) | async-done | bytes 67108880 | tf_op jit(solution)/shard_map/all_gather | solution.py:35
  2769.8 79.4 %fusion.36 = f32[8192,1024]{1,0:T(8,128)} fusion(bf16[4096,8192]{1,0:T(8,128)(2,1)} %all-gather.9.cloned.1.call-done, bf16[4096,1024]{1,0:T(8,128)(2,1)} %param.15), kind=kOutput, calls=%fused_computation.63 | convolution fusion | flops 68719476736 | bytes 109051904 | tf_op jit(solution)/shard_map/dot_general | solution.py:42
  2849.2 0.0 copy-start.7
  2849.2 0.0 copy-start.1
  2849.2 0.0 copy-start.3
  2849.2 0.0 copy-start.4
  2849.3 0.0 reduce-scatter.11.cloned.1.call-update
  2849.3 0.6 copy-done.7
  2849.9 148.4 %reduce-scatter.9.cloned.1.call-done = f32[512,4096]{1,0:T(8,128)} async-done(((f32[2048,4096]{1,0:T(8,128)}), f32[512,4096]{1,0:T(8,128)}) %reduce-scatter.9.cloned.1.call-update) | async-done | bytes 8388624 | tf_op jit(solution)/shard_map/reduce_scatter | solution.py:46
  2998.3 6.0 convert_element_type.53
  3004.3 362.3 %reduce-scatter.7.cloned.1.call-done = f32[4096,1024]{1,0:T(8,128)} async-done(((f32[4096,2048]{1,0:T(8,128)}), f32[4096,1024]{1,0:T(8,128)}) %reduce-scatter.7.cloned.1.call-update) | async-done | bytes 16777232 | tf_op jit(solution)/shard_map/reduce_scatter | solution.py:49
  3366.7 0.0 copy-done.1
  3366.7 0.0 copy-done.3
  3366.7 0.0 copy-done.4
  3366.7 11.0 fusion.27
  3377.8 7.5 psum.36
  3385.3 0.0 copy-start.5
  3385.3 16.2 convert_reduce_fusion.2
  3401.5 0.0 copy-done.5
  3401.5 10.9 all-reduce
  3412.4 0.6 fusion.32
  3413.0 80.0 %fusion.29 = bf16[4096,1024]{1,0:T(8,128)(2,1)} fusion(bf16[4096,1024]{1,0:T(8,128)(2,1)} %param.8, bf16[4096,8192]{1,0:T(8,128)(2,1)} %all-gather.9.cloned.1.call-done, bf16[8192,1024]{1,0:T(8,128)(2,1)} %all-gather.11.cloned.1.call-done, f32[1024]{0:T(1024)S(1)} %convert_element_type.48), kind=kOutput, calls=%fused_computation.48 | convolution fusion | flops 68736253952 | bytes 100667392 | tf_op jit(solution)/shard_map/dot_general | solution.py:37
  3493.0 102.3 %reduce-scatter.11.cloned.1.call-done = f32[2048,1024]{1,0:T(8,128)} async-done(((f32[8192,1024]{1,0:T(8,128)}), f32[2048,1024]{1,0:T(8,128)}) %reduce-scatter.11.cloned.1.call-update) | async-done | bytes 8388624 | tf_op jit(solution)/shard_map/reduce_scatter | solution.py:43
  3595.3 6.1 convert_element_type.55
  (7 shorter events, 0.2 us)
Async XLA Ops:
  7.2 109.4 %all-gather.11.cloned.1.call-start = ((), (), s32[]{:S(2)}) async-start(), calls=%async_computation.7 | async-start | bytes 20971520 | tf_op jit(solution)/shard_map/all_gather | solution.py:36
  7.9 307.5 %all-gather.5.cloned.1.call-start = ((), (), s32[]{:S(2)}) async-start(), calls=%async_computation.4 | async-start | bytes 25165824 | tf_op jit(solution)/shard_map/all_gather | solution.py:30
  24.2 0.6 copy-start
  24.2 0.6 copy-start.2
  33.3 387.8 %all-gather.7.cloned.1.call-start = ((), (), s32[]{:S(2)}) async-start(), calls=%async_computation.5 | async-start | bytes 20971520 | tf_op jit(solution)/shard_map/all_gather | solution.py:31
  34.0 1833.9 %reduce-scatter.5.cloned.1.call-start = ((), (), s32[]{:S(2)}) async-start(), calls=%async_computation.8 | async-start | bytes 201326592 | tf_op jit(solution)/shard_map/reduce_scatter | solution.py:40
  197.9 0.7 copy-start.6
  197.9 2571.9 %all-gather.9.cloned.1.call-start = ((), (), s32[]{:S(2)}) async-start(), calls=%async_computation.6 | async-start | bytes 100663296 | tf_op jit(solution)/shard_map/all_gather | solution.py:35
  2006.5 991.8 %reduce-scatter.9.cloned.1.call-start = ((), (), s32[]{:S(2)}) async-start(), calls=%async_computation.10 | async-start | bytes 41943040 | tf_op jit(solution)/shard_map/reduce_scatter | solution.py:46
  2096.7 1270.0 %reduce-scatter.7.cloned.1.call-start = ((), (), s32[]{:S(2)}) async-start(), calls=%async_computation.9 | async-start | bytes 50331648 | tf_op jit(solution)/shard_map/reduce_scatter | solution.py:49
  2175.3 1420.0 %reduce-scatter.11.cloned.1.call-start = ((), (), s32[]{:S(2)}) async-start(), calls=%async_computation.11 | async-start | bytes 41943040 | tf_op jit(solution)/shard_map/reduce_scatter | solution.py:43
  2849.2 0.7 copy-start.7
  2849.2 517.4 %copy-start.1 = (f32[4096,1]{0,1:T(1,128)S(1)}, f32[4096,1]{0,1:T(1,128)}, u32[]{:S(2)}) copy-start(f32[4096,1]{0,1:T(1,128)} %copy-done) | copy-start | bytes 49156
  2849.2 517.4 %copy-start.3 = (f32[4096,1]{0,1:T(1,128)S(1)}, f32[4096,1]{0,1:T(1,128)}, u32[]{:S(2)}) copy-start(f32[4096,1]{0,1:T(1,128)} %copy-done.2) | copy-start | bytes 49156
  2849.2 517.4 %copy-start.4 = (f32[1024]{0:T(1024)S(1)}, f32[1024]{0:T(1024)}, u32[]{:S(2)}) copy-start(f32[1024]{0:T(1024)} %param.9) | copy-start | bytes 12292
  3385.3 16.2 copy-start.5
Sparse Core Ops, SparseCore 0:
  9.5 107.0 all-gather.10
  118.6 196.6 all-gather.4
  316.9 104.1 all-gather.6
  423.2 1444.6 reduce-scatter.4
  2006.7 763.1 all-gather.8
  2772.2 226.0 reduce-scatter.8
  3000.6 366.0 reduce-scatter.6
  3369.2 225.9 reduce-scatter.10
where the time goes:
time: 3610 us
  waiting for transfers between devices  2960 us (82%)
  matrix products  537 us (15%)
  other arithmetic  53.7 us (1%)
    reduce_scatter x1, waiting for transfers between devices, local_step(): d_act = lax.psum_scatter(da_part, 'col', scatter_dimension=1, tiled=True)  1450 us
    all_gather x1, waiting for transfers between devices, local_step(): a_rows = lax.all_gather(a_act, 'col', axis=1, tiled=True)  594 us
    reduce_scatter x1, waiting for transfers between devices, local_step(): dz_act = lax.psum_scatter(dz_part, 'col', scatter_dimension=1, tiled=True)  362 us
    reduce_scatter x1, waiting for transfers between devices, local_step(): lax.psum_scatter(dwu_part, 'row', scatter_dimension=0, tiled=True)  148 us
    dot_general x1, matrix products, local_step(): jnp.dot(z_rows, w_up_cols, preferred_element_type=jnp.float32)  139 us
    all_gather x1, waiting for transfers between devices, local_step(): z_rows = lax.all_gather(z_act, 'col', axis=1, tiled=True)  117 us
    all_gather x1, waiting for transfers between devices, local_step(): w_up_cols = lax.all_gather(w_up, 'row', axis=0, tiled=True)  106 us
    reduce_scatter x1, waiting for transfers between devices, local_step(): lax.psum_scatter(dwd_part, 'row', scatter_dimension=0, tiled=True)  102 us
  transfers between devices with their start and end apart: 8, of which 8 were waited for; matrix products, arithmetic and copies ran while one was open for 12% of the time, Pallas kernels for 0%

commit v1 on v0

v1 whole, which is shorter than its diff:
```python
import jax
import jax.numpy as jnp
from jax import lax
from jax.experimental import pallas as pl
from jax.experimental.pallas import tpu as pltpu
from jax.sharding import PartitionSpec as P


LN_EPS = 1e-5
GELU_K = 0.7978845608028654
GELU_A = 0.044715
CONTRACT_ROWS = (((0,), (0,)), ((), ()))
CONTRACT_COLS = (((1,), (1,)), ((), ()))
CONTRACT_MM = (((1,), (0,)), ((), ()))
NX = 4
NDY = 2
SUB = 256
VMEM = 58 * 1024 * 1024


def half_sigmoid(u_val, sq):
    return 0.5 + 0.5 * jnp.tanh(u_val * (GELU_K + (GELU_K * GELU_A) * sq))


def gelu_grad(u_val):
    sq = u_val * u_val
    half = half_sigmoid(u_val, sq)
    return half + (half * (1.0 - half) * u_val) * (2.0 * GELU_K + (6.0 * GELU_K * GELU_A) * sq)


def dot32(a, b, dims=CONTRACT_MM):
    return lax.dot_general(a, b, dims, preferred_element_type=jnp.float32)


def ln_kernel(c_ref, xl_ref, xr_ref, g_ref, b_ref, *refs):
    z_ref, st_ref = refs[-2:]
    width = xl_ref.shape[1]
    first = c_ref[0] == 0
    xl = xl_ref[...].astype(jnp.float32)
    xr = xr_ref[...].astype(jnp.float32)
    total = jnp.sum(xl, axis=1, keepdims=True) + jnp.sum(xr, axis=1, keepdims=True)
    square = jnp.sum(xl * xl, axis=1, keepdims=True) + jnp.sum(xr * xr, axis=1, keepdims=True)
    mean = total / (2 * width)
    inv = lax.rsqrt(square / (2 * width) - mean * mean + LN_EPS)
    hl = (xl - mean) * inv
    hr = (xr - mean) * inv
    lo = jnp.where(first, hl, hr)
    hi = jnp.where(first, hr, hl)
    z_ref[:, :width] = (lo * g_ref[:, :width] + b_ref[:, :width]).astype(z_ref.dtype)
    z_ref[:, width:] = (hi * g_ref[:, width:] + b_ref[:, width:]).astype(z_ref.dtype)
    lane = lax.broadcasted_iota(jnp.int32, st_ref.shape, 1)
    st_ref[...] = jnp.where(lane == 0, mean, inv)


def ln_call(cvec, x_in, x_rem, gain, bias, k, z_buf):
    rows, width = x_rem.shape
    tokens = x_in.shape[0]
    bm = 256
    off = k * rows // bm
    in_specs = [
        pl.BlockSpec((bm, width), lambda i, c: (off + i, 0)),
        pl.BlockSpec((bm, width), lambda i, c: (i, 0)),
        pl.BlockSpec((1, 2 * width), lambda i, c: (0, 0)),
        pl.BlockSpec((1, 2 * width), lambda i, c: (0, 0)),
    ]
    args = [cvec, x_in, x_rem, gain, bias]
    alias = {}
    if z_buf is not None:
        in_specs.append(pl.BlockSpec(memory_space=pl.ANY))
        args.append(z_buf)
        alias = {5: 0}
    return pl.pallas_call(
        ln_kernel,
        grid_spec=pltpu.PrefetchScalarGridSpec(
            num_scalar_prefetch=1,
            grid=(rows // bm,),
            in_specs=in_specs,
            out_specs=[
                pl.BlockSpec((bm, 2 * width), lambda i, c: (off + i, 0)),
                pl.BlockSpec((bm, 128), lambda i, c: (i, 0)),
            ],
        ),
        out_shape=[
            jax.ShapeDtypeStruct((tokens, 2 * width), jnp.bfloat16),
            jax.ShapeDtypeStruct((rows, 128), jnp.float32),
        ],
        input_output_aliases=alias,
        compiler_params=pltpu.CompilerParams(vmem_limit_bytes=VMEM),
        cost_estimate=pl.CostEstimate(flops=rows * width * 400, bytes_accessed=rows * width * 8, transcendentals=0),
    )(*args)


def ua_kernel(c_ref, z_ref, w_ref, b_ref, *refs):
    u_ref, a_ref = refs[-2:]
    for i in range(z_ref.shape[0] // SUB):
        part = pl.ds(i * SUB, SUB)
        u = (dot32(z_ref[part, :], w_ref[...]) + b_ref[...]).astype(u_ref.dtype)
        u_ref[part, :] = u
        u32 = u.astype(jnp.float32)
        a_ref[part, :] = (u32 * half_sigmoid(u32, u32 * u32)).astype(a_ref.dtype)


def ua_call(cvec, z_buf, w_half, b_half, k, other, bufs):
    tokens, width = z_buf.shape
    ffh = w_half.shape[1]
    rows = tokens // NX
    bn = 512
    nb = ffh // bn

    def col(j, c):
        return ((1 - c[0]) if other else c[0]) * nb + j

    in_specs = [
        pl.BlockSpec((rows, width), lambda j, c: (k, 0)),
        pl.BlockSpec((width, bn), lambda j, c: (0, j)),
        pl.BlockSpec((1, bn), lambda j, c: (0, j)),
    ]
    args = [cvec, z_buf, w_half, b_half]
    alias = {}
    if bufs is not None:
        in_specs += [pl.BlockSpec(memory_space=pl.ANY)] * 2
        args += list(bufs)
        alias = {4: 0, 5: 1}
    out = pl.BlockSpec((rows, bn), lambda j, c: (k, col(j, c)))
    shape = jax.ShapeDtypeStruct((tokens, 2 * ffh), jnp.bfloat16)
    return pl.pallas_call(
        ua_kernel,
        grid_spec=pltpu.PrefetchScalarGridSpec(
            num_scalar_prefetch=1, grid=(nb,), in_specs=in_specs, out_specs=[out, out]),
        out_shape=[shape, shape],
        input_output_aliases=alias,
        compiler_params=pltpu.CompilerParams(vmem_limit_bytes=VMEM),
        cost_estimate=pl.CostEstimate(
            flops=2 * rows * width * ffh, bytes_accessed=2 * (rows * width + width * ffh + 2 * rows * ffh),
            transcendentals=rows * ffh),
    )(*args)


def du_kernel(c_ref, yl_ref, yr_ref, wl_ref, wr_ref, u_ref, *refs):
    du_ref, sum_ref = refs[-2:]
    total = jnp.zeros(sum_ref.shape, jnp.float32)
    for i in range(yl_ref.shape[0] // SUB):
        part = pl.ds(i * SUB, SUB)
        da = dot32(yl_ref[part, :], wl_ref[...], CONTRACT_COLS) + dot32(yr_ref[part, :], wr_ref[...], CONTRACT_COLS)
        du = (da * gelu_grad(u_ref[part, :].astype(jnp.float32))).astype(du_ref.dtype)
        du_ref[part, :] = du
        total += jnp.sum(du.astype(jnp.float32).reshape(SUB // 8, 8, -1), axis=0)
    sum_ref[...] = total


def du_call(cvec, dy_out, dy_rem, w_own, w_oth, u_buf, k, other, buf):
    tokens, dloc = dy_out.shape
    rows = dy_rem.shape[0]
    ffh = w_own.shape[0] // 2
    bn = 512
    nb = ffh // bn

    def off(j, c):
        return ((1 - c[0]) if other else c[0]) * nb + j

    in_specs = [
        pl.BlockSpec((rows, dloc), lambda j, c: (k, 0)),
        pl.BlockSpec((rows, dloc), lambda j, c: (0, 0)),
        pl.BlockSpec((bn, dloc), lambda j, c: (off(j, c), 0)),
        pl.BlockSpec((bn, dloc), lambda j, c: (off(j, c), 0)),
        pl.BlockSpec((rows, bn), lambda j, c: (k, off(j, c))),
    ]
    args = [cvec, dy_out, dy_rem, w_own, w_oth, u_buf]
    alias = {}
    if buf is not None:
        in_specs.append(pl.BlockSpec(memory_space=pl.ANY))
        args.append(buf)
        alias = {6: 0}
    return pl.pallas_call(
        du_kernel,
        grid_spec=pltpu.PrefetchScalarGridSpec(
            num_scalar_prefetch=1, grid=(nb,), in_specs=in_specs,
            out_specs=[
                pl.BlockSpec((rows, bn), lambda j, c: (k, j)),
                pl.BlockSpec((8, bn), lambda j, c: (0, j)),
            ]),
        out_shape=[
            jax.ShapeDtypeStruct((tokens, ffh), jnp.bfloat16),
            jax.ShapeDtypeStruct((8, ffh), jnp.float32),
        ],
        input_output_aliases=alias,
        compiler_params=pltpu.CompilerParams(vmem_limit_bytes=VMEM),
        cost_estimate=pl.CostEstimate(
            flops=4 * rows * dloc * ffh, bytes_accessed=4 * (rows * dloc + dloc * ffh + rows * ffh),
            transcendentals=rows * ffh),
    )(*args)


def solution(mesh):
    swap = [(0, 1), (1, 0)]
    barrier = lax.optimization_barrier

    def swap_col(v):
        return lax.ppermute(v, 'col', swap)

    def gather_row(v):
        return lax.all_gather(v, 'row', axis=0, tiled=True)

    def local_step(x_in, ln_gain, ln_bias, w_up, b_up, w_down, b_down, dy_out):
        cid = lax.axis_index('col')
        cvec = jnp.full((1,), cid, jnp.int32)
        first = cid == 0
        tokens, dloc = x_in.shape
        width = dloc * mesh.shape['col']
        ffh = w_up.shape[1]
        xrows = tokens // NX
        yrows = tokens // NDY

        pieces = [x_in[k * xrows:(k + 1) * xrows] for k in range(NX)]
        pieces += [dy_out[k * yrows:(k + 1) * yrows] for k in range(NDY)]
        pieces = barrier(pieces)
        vecs = jnp.concatenate([ln_gain, ln_bias, b_up.astype(jnp.float32)])
        vecs_o = swap_col(vecs)
        w_up_sw = swap_col(w_up)
        x_o = [swap_col(v) for v in pieces[:NX]]
        w_dn_sw = swap_col(w_down)
        dy_o = [swap_col(v) for v in pieces[NX:]]
        w1_own = gather_row(w_up)
        w1_oth = gather_row(w_up_sw)
        w2_own = gather_row(w_down)
        db_loc = barrier(sum(jnp.sum(v.astype(jnp.float32), axis=0) for v in pieces[NX:]))

        def true_cols(own, oth):
            return jnp.concatenate([jnp.where(first, own, oth), jnp.where(first, oth, own)], axis=-1)[None]

        gain = true_cols(vecs[:dloc], vecs_o[:dloc])
        bias = true_cols(vecs[dloc:2 * dloc], vecs_o[dloc:2 * dloc])
        w1 = (w1_own, w1_oth)
        b1 = (vecs[None, 2 * dloc:], vecs_o[None, 2 * dloc:])

        z_buf, bufs, stats = None, None, []
        for k in range(NX):
            if bufs is not None:
                x_o[k], bufs, z_buf = barrier((x_o[k], bufs, z_buf))
            z_buf, st = ln_call(cvec, x_in, x_o[k], gain, bias, k, z_buf)
            stats.append(st)
            todo = [(k, 0)] + ([(k - 1, 1)] if k else []) + ([(k, 1)] if k == NX - 1 else [])
            for piece, other in todo:
                bufs = ua_call(cvec, z_buf, w1[other], b1[other], piece, other, bufs)
        w_dn_sw, bufs = barrier((w_dn_sw, bufs))
        u_buf, a_buf = bufs
        w2_oth = gather_row(w_dn_sw)

        dw2 = dot32(a_buf, dy_out, CONTRACT_ROWS)
        w2_own, dw2 = barrier((w2_own, dw2))
        dw_down = lax.psum_scatter(dw2, 'row', scatter_dimension=0, tiled=True).astype(jnp.bfloat16)
        x_f32 = x_in.astype(jnp.float32)
        y_sum = dot32(a_buf, w2_own)
        y_out = (x_f32 + y_sum + b_down.astype(jnp.float32)).astype(jnp.bfloat16)
        dy_o[0], y_out = barrier((dy_o[0], y_out))

        def du_half(other):
            buf, sums = None, []
            for k in range(NDY):
                buf, part = du_call(cvec, dy_out, dy_o[k], w2_own, w2_oth, u_buf, k, other, buf)
                sums.append(part)
            return buf, sum(sums)

        du_own, sum_own = du_half(0)
        db_up = jnp.sum(sum_own, axis=0)
        dwu = dot32(z_buf, du_own, CONTRACT_ROWS)
        dwu, u_buf = barrier((dwu, u_buf))
        dw_up = lax.psum_scatter(dwu, 'row', scatter_dimension=0, tiled=True).astype(jnp.bfloat16)
        du_oth, _ = du_half(1)

        w1_own_r = lax.dynamic_slice_in_dim(w1_own, cid * dloc, dloc, 0)
        w1_oth_r = lax.dynamic_slice_in_dim(w1_oth, cid * dloc, dloc, 0)
        dz = dot32(du_own, w1_own_r, CONTRACT_COLS) + dot32(du_oth, w1_oth_r, CONTRACT_COLS)

        st = jnp.concatenate(stats, axis=0)
        mean_x, inv_std = st[:, 0:1], st[:, 1:2]
        x_hat = (x_f32 - mean_x) * inv_std
        value_a6 = dz * ln_gain
        row_sums = jnp.concatenate([jnp.sum(value_a6, axis=1, keepdims=True), jnp.sum(value_a6 * x_hat, axis=1, keepdims=True)], axis=1)
        row_sums = lax.psum(row_sums, 'col')
        sums = lax.psum(jnp.concatenate([db_up, db_loc, jnp.sum(dz * x_hat, axis=0), jnp.sum(dz, axis=0)]), 'row')
        mean_dxh = row_sums[:, 0:1] / width
        mean_dxh_xh = row_sums[:, 1:2] / width
        dx_in = (dy_out.astype(jnp.float32) + inv_std * (value_a6 - mean_dxh - x_hat * mean_dxh_xh)).astype(jnp.bfloat16)
        db_up, db_down, d_gain, d_bias = sums[:ffh], sums[ffh:ffh + dloc], sums[ffh + dloc:ffh + 2 * dloc], sums[ffh + 2 * dloc:]
        return (y_out, dx_in, dw_up, db_up, dw_down, db_down, d_gain, d_bias)

    blk_spec = P('row', 'col')
    vec_spec = P('col')
    return jax.shard_map(local_step, mesh=mesh, in_specs=(blk_spec, vec_spec, vec_spec, blk_spec, vec_spec, blk_spec, vec_spec, blk_spec), out_specs=(blk_spec, blk_spec, blk_spec, vec_spec, blk_spec, vec_spec, vec_spec, vec_spec), check_vma=False)
```

time: 3610 us -> 1190 us (0.33)
  waiting for transfers between devices: 2960 us -> 255 us
  Pallas kernels: 0 us -> 479 us
  matrix products: 537 us -> 344 us
    reduce_scatter x4 -> x2, waiting for transfers between devices: 2060 us -> 0.01 us  [the longest x1 0.01 us: local_step(): lax.psum_scatter(dw2, 'row', scatter_dimension=0, tiled=True)]
    all_gather x4, waiting for transfers between devices: 899 us -> 0.01 us  [gather_row(): return lax.all_gather(v, 'row', axis=0, tiled=True)]
    pallas_call x0 -> x16, Pallas kernels: none -> 479 us  [the longest x4 230 us: du_call(): pl.pallas_call(du_kernel, grid_spec=pltpu.PrefetchScalarGridSpec(num_scal...]
    ppermute x0 -> x9, waiting for transfers between devices: none -> 254 us  [swap_col(): return lax.ppermute(v, 'col', swap)]
    dot_general x6 -> x5, matrix products: 537 us -> 344 us  [dot32(): return lax.dot_general(a, b, dims, preferred_element_type=jnp.float32)]
  transfers between devices with their start and end apart: 8 -> 15, of which waited for: 8 -> 5; matrix products, arithmetic and copies ran while one was open for 12% -> 33% of each run, Pallas kernels for 0% -> 41%
where the time goes in v1:
time: 1190 us; the launch traced here: 1180 us
  Pallas kernels  479 us (40%)
  matrix products  344 us (29%)
  waiting for transfers between devices  255 us (21%)
  other arithmetic  35.4 us (3%)
  blocking collectives  19.2 us (2%)
  local copies, waits for them, and re-layouts  17.7 us (1%)
  between operations  14.5 us (1%)
  starting transfers between devices  13.1 us (1%)
    dot_general x5, matrix products, dot32(): return lax.dot_general(a, b, dims, preferred_element_type=jnp.float32)  344 us
    ppermute x9, waiting for transfers between devices, swap_col(): return lax.ppermute(v, 'col', swap)  254 us
    pallas_call x4, Pallas kernels, du_call(): pl.pallas_call(du_kernel, grid_spec=pltpu.PrefetchScalarGridSpec(num_scal...  230 us
    pallas_call x8, Pallas kernels, ua_call(): pl.pallas_call(ua_kernel, grid_spec=pltpu.PrefetchScalarGridSpec(num_scal...  224 us
    pallas_call x4, Pallas kernels, ln_call(): pl.pallas_call(ln_kernel, grid_spec=pltpu.PrefetchScalarGridSpec(num_scal...  25.3 us
  transfers between devices with their start and end apart: 15, of which 5 were waited for; matrix products, arithmetic and copies ran while one was open for 33% of the time, Pallas kernels for 41%

profile of v1, /device:TPU:0, one launch (start us, length us, event | category | flops | bytes accessed | tf_op | source)
XLA Modules:
  0.0 1179.1 jit_solution(9551951619947147582)
XLA Ops:
  7.2 0.0 all-gather.5.cloned.1.call-start
  7.2 0.7 all-gather.5.cloned.1.call-update
  7.9 0.0 all-gather.7.cloned.1.call-start
  7.9 3.4 collective-permute-start.7
  11.3 90.9 %collective-permute-done.7 = bf16[512,4096]{1,0:T(8,128)(2,1)} collective-permute-done((bf16[512,4096]{1,0:T(8,128)(2,1)}, bf16[512,4096]{1,0:T(8,128)(2,1)}, u32[]{:S(2)}, u32[]{:S(2)}) %collective-permute-start.7) | collective-permute-done | bytes 4194336 | tf_op jit(solution)/shard_map/ppermute | solution.py:199
  102.2 0.0 all-gather.7.cloned.1.call-update
  102.2 0.0 all-gather.9.cloned.1.call-start
  102.3 0.7 all-gather.9.cloned.1.call-update
  103.0 0.0 all-gather.11.cloned.1.call-start
  103.0 6.6 fusion.18
  109.6 2.3 copy-done
  111.9 3.8 fusion.17
  115.7 1.7 collective-permute-start.5
  117.4 0.4 collective-permute-start.4
  117.7 1.7 collective-permute-start.6
  119.4 0.4 collective-permute-start.1
  119.8 1.7 collective-permute-start.3
  121.5 88.4 %collective-permute-done.6 = f32[6144]{0:T(1024)S(1)} collective-permute-done((f32[6144]{0:T(1024)S(1)}, f32[6144]{0:T(1024)S(1)}, u32[]{:S(2)}, u32[]{:S(2)}) %collective-permute-start.6) | collective-permute-done | bytes 24608 | tf_op jit(solution)/shard_map/ppermute | solution.py:199
  209.9 1.7 collective-permute-start.2
  211.5 0.6 slice.70
  212.1 0.6 pad_maximum_fusion.3
  212.8 1.4 copy-done.1
  214.1 6.3 shard_map.143
  220.4 27.9 %shard_map.144 = (bf16[4096,8192]{1,0:T(8,128)(2,1)}, bf16[4096,8192]{1,0:T(8,128)(2,1)}) custom-call(s32[1]{0:T(128)} %bitcast.c_ref, bf16[4096,2048]{1,0:T(8,128)(2,1)} %get-tuple-element.74.z_ref.refs_0_, bf16[2048,4096]{1,0:T(8,128)(2,1)} %all-gather.5.cloned.1.call-done.w_ref, f32[1,4096]{1,0:T(1,128)} %bitcast.21), custom_call_target="tpu_custom_call" | custom-call | flops 17179869184 | bytes 37748736 | tf_op jit(solution)/shard_map/pallas_call | solution.py:126
  248.3 6.4 shard_map.145
  254.8 28.1 %shard_map.146 = (bf16[4096,8192]{1,0:T(8,128)(2,1)}, bf16[4096,8192]{1,0:T(8,128)(2,1)}) custom-call(s32[1]{0:T(128)} %bitcast.c_ref, bf16[4096,2048]{1,0:T(8,128)(2,1)} %get-tuple-element.83.z_ref.refs_0_, bf16[2048,4096]{1,0:T(8,128)(2,1)} %all-gather.5.cloned.1.call-done.w_ref, ...), custom_call_target="tpu_custom_call", output_to_operand_aliasing={{0}: (4, {}), {1}: (5, {})} | custom-call | flops 17179869184 | bytes 37748736 | tf_op jit(solution)/shard_map/pallas_call | solution.py:126
  282.9 27.9 %shard_map.147 = (bf16[4096,8192]{1,0:T(8,128)(2,1)}, bf16[4096,8192]{1,0:T(8,128)(2,1)}) custom-call(s32[1]{0:T(128)} %bitcast.c_ref, bf16[4096,2048]{1,0:T(8,128)(2,1)} %get-tuple-element.83.z_ref.refs_0_, bf16[2048,4096]{1,0:T(8,128)(2,1)} %all-gather.7.cloned.1.call-done.w_ref, ...), custom_call_target="tpu_custom_call", output_to_operand_aliasing={{0}: (4, {}), {1}: (5, {})} | custom-call | flops 17179869184 | bytes 37748736 | tf_op jit(solution)/shard_map/pallas_call | solution.py:126
  310.8 34.0 %collective-permute-done.3.xr_ref = bf16[1024,1024]{1,0:T(8,128)(2,1)} collective-permute-done((bf16[1024,1024]{1,0:T(8,128)(2,1)}, bf16[1024,1024]{1,0:T(8,128)(2,1)}, u32[]{:S(2)}, u32[]{:S(2)}) %collective-permute-start.3) | collective-permute-done | bytes 2097184 | tf_op jit(solution)/shard_map/ppermute | solution.py:199
  344.8 6.3 shard_map.148
  351.1 28.3 %shard_map.149 = (bf16[4096,8192]{1,0:T(8,128)(2,1)}, bf16[4096,8192]{1,0:T(8,128)(2,1)}) custom-call(s32[1]{0:T(128)} %bitcast.c_ref, bf16[4096,2048]{1,0:T(8,128)(2,1)} %get-tuple-element.92.z_ref.refs_0_, bf16[2048,4096]{1,0:T(8,128)(2,1)} %all-gather.5.cloned.1.call-done.w_ref, ...), custom_call_target="tpu_custom_call", output_to_operand_aliasing={{0}: (4, {}), {1}: (5, {})} | custom-call | flops 17179869184 | bytes 37748736 | tf_op jit(solution)/shard_map/pallas_call | solution.py:126
  379.4 27.9 %shard_map.150 = (bf16[4096,8192]{1,0:T(8,128)(2,1)}, bf16[4096,8192]{1,0:T(8,128)(2,1)}) custom-call(s32[1]{0:T(128)} %bitcast.c_ref, bf16[4096,2048]{1,0:T(8,128)(2,1)} %get-tuple-element.92.z_ref.refs_0_, bf16[2048,4096]{1,0:T(8,128)(2,1)} %all-gather.7.cloned.1.call-done.w_ref, ...), custom_call_target="tpu_custom_call", output_to_operand_aliasing={{0}: (4, {}), {1}: (5, {})} | custom-call | flops 17179869184 | bytes 37748736 | tf_op jit(solution)/shard_map/pallas_call | solution.py:126
  407.2 6.3 shard_map.151
  413.6 27.9 %shard_map.152 = (bf16[4096,8192]{1,0:T(8,128)(2,1)}, bf16[4096,8192]{1,0:T(8,128)(2,1)}) custom-call(s32[1]{0:T(128)} %bitcast.c_ref, bf16[4096,2048]{1,0:T(8,128)(2,1)} %get-tuple-element.93.z_ref, bf16[2048,4096]{1,0:T(8,128)(2,1)} %all-gather.5.cloned.1.call-done.w_ref, f32[1,4096]{1,0:T(1,128)} %bitcast.24, ...), custom_call_target="tpu_custom_call", output_to_operand_aliasing={{0}: (4, {}), {1}: (5, {})} | custom-call | flops 17179869184 | bytes 37748736 | tf_op jit(solution)/shard_map/pallas_call | solution.py:126
  441.4 27.8 %shard_map.153 = (bf16[4096,8192]{1,0:T(8,128)(2,1)}, bf16[4096,8192]{1,0:T(8,128)(2,1)}) custom-call(s32[1]{0:T(128)} %bitcast.c_ref, bf16[4096,2048]{1,0:T(8,128)(2,1)} %get-tuple-element.93.z_ref, bf16[2048,4096]{1,0:T(8,128)(2,1)} %all-gather.7.cloned.1.call-done.w_ref, f32[1,4096]{1,0:T(1,128)} %bitcast.19, ...), custom_call_target="tpu_custom_call", output_to_operand_aliasing={{0}: (4, {}), {1}: (5, {})} | custom-call | flops 17179869184 | bytes 37748736 | tf_op jit(solution)/shard_map/pallas_call | solution.py:126
  469.2 27.8 %shard_map.154 = (bf16[4096,8192]{1,0:T(8,128)(2,1)}, bf16[4096,8192]{1,0:T(8,128)(2,1)}) custom-call(s32[1]{0:T(128)} %bitcast.c_ref, bf16[4096,2048]{1,0:T(8,128)(2,1)} %get-tuple-element.93.z_ref, bf16[2048,4096]{1,0:T(8,128)(2,1)} %all-gather.7.cloned.1.call-done.w_ref, f32[1,4096]{1,0:T(1,128)} %bitcast.20, ...), custom_call_target="tpu_custom_call", output_to_operand_aliasing={{0}: (4, {}), {1}: (5, {})} | custom-call | flops 17179869184 | bytes 37748736 | tf_op jit(solution)/shard_map/pallas_call | solution.py:126
  497.1 0.0 all-gather.11.cloned.1.call-update
  497.1 0.0 reduce-scatter.5.cloned.1.call-start
  497.1 92.7 %fusion.20 = f32[8192,1024]{1,0:T(8,128)} fusion(bf16[4096,8192]{1,0:T(8,128)(2,1)} %get-tuple-element.102, bf16[4096,1024]{1,0:T(8,128)(2,1)} %yl_ref.7), kind=kOutput, calls=%fused_computation.44 | convolution fusion | flops 68719476736 | bytes 109051904 | tf_op jit(solution)/shard_map/dot_general | solution.py:32
  589.9 0.0 reduce-scatter.5.cloned.1.call-update
  589.9 0.0 reduce-scatter.3.cloned.1.call-start
  589.9 1.8 collective-permute-start
  591.8 0.2 collective-permute-start.8
  592.0 80.0 %fusion.1 = bf16[4096,1024]{1,0:T(8,128)(2,1)} fusion(bf16[4096,1024]{1,0:T(8,128)(2,1)} %xl_ref.7, bf16[4096,8192]{1,0:T(8,128)(2,1)} %get-tuple-element.102, bf16[8192,1024]{1,0:T(8,128)(2,1)} %all-gather.9.cloned.1.call-done.wl_ref, f32[1024]{0:T(1024)S(1)} %convert_element_type.32), kind=kOutput, calls=%fused_computation.3 | convolution fusion | flops 68736253952 | bytes 100667392 | tf_op jit(solution)/shard_map/dot_general | solution.py:32
  672.0 11.7 collective-permute-done.yr_ref
  683.7 57.1 %shard_map.155 = (bf16[4096,4096]{1,0:T(8,128)(2,1)}, f32[8,4096]{1,0:T(8,128)}) custom-call(s32[1]{0:T(128)} %bitcast.c_ref, bf16[4096,1024]{1,0:T(8,128)(2,1)} %yl_ref.7, bf16[2048,1024]{1,0:T(8,128)(2,1)} %collective-permute-done.yr_ref, bf16[8192,1024]{1,0:T(8,128)(2,1)} %all-gather.9.cloned.1.call-done.wl_ref, ...), custom_call_target="tpu_custom_call" | custom-call | flops 34359738368 | bytes 58720256 | tf_op jit(solution)/shard_map/pallas_call | solution.py:174
  740.8 29.0 %collective-permute-done.8.yr_ref = bf16[2048,1024]{1,0:T(8,128)(2,1)} collective-permute-done((bf16[2048,1024]{1,0:T(8,128)(2,1)}, bf16[2048,1024]{1,0:T(8,128)(2,1)}, u32[]{:S(2)}, u32[]{:S(2)}) %collective-permute-start.8) | collective-permute-done | bytes 4194336 | tf_op jit(solution)/shard_map/ppermute | solution.py:199
  769.8 56.4 %shard_map.156 = (bf16[4096,4096]{1,0:T(8,128)(2,1)}, f32[8,4096]{1,0:T(8,128)}) custom-call(s32[1]{0:T(128)} %bitcast.c_ref, bf16[4096,1024]{1,0:T(8,128)(2,1)} %yl_ref.7, bf16[2048,1024]{1,0:T(8,128)(2,1)} %collective-permute-done.8.yr_ref, bf16[8192,1024]{1,0:T(8,128)(2,1)} %all-gather.9.cloned.1.call-done.wl_ref, ...), custom_call_target="tpu_custom_call", output_to_operand_aliasing={{0}: (6, {})} | custom-call | flops 34359738368 | bytes 58720256 | tf_op jit(solution)/shard_map/pallas_call | solution.py:174
  826.2 79.6 %fusion.21 = f32[2048,4096]{1,0:T(8,128)} fusion(bf16[4096,2048]{1,0:T(8,128)(2,1)} %get-tuple-element.93.z_ref, bf16[4096,4096]{1,0:T(8,128)(2,1)} %get-tuple-element.114), kind=kOutput, calls=%fused_computation.45 | convolution fusion | flops 68719476736 | bytes 83886080 | tf_op jit(solution)/shard_map/dot_general | solution.py:32
  905.8 0.0 reduce-scatter.3.cloned.1.call-update
  905.8 5.6 convert_reduce_fusion
  911.5 0.6 add.42
  912.3 1.7 slice_reduce_fusion.1
  914.0 0.6 add_reduce_fusion
  914.6 60.3 %shard_map.157 = (bf16[4096,4096]{1,0:T(8,128)(2,1)}, f32[8,4096]{1,0:T(8,128)}) custom-call(s32[1]{0:T(128)} %bitcast.c_ref, bf16[4096,1024]{1,0:T(8,128)(2,1)} %yl_ref.7, bf16[2048,1024]{1,0:T(8,128)(2,1)} %collective-permute-done.yr_ref, bf16[8192,1024]{1,0:T(8,128)(2,1)} %all-gather.9.cloned.1.call-done.wl_ref, ...), custom_call_target="tpu_custom_call" | custom-call | flops 34359738368 | bytes 58720256 | tf_op jit(solution)/shard_map/pallas_call | solution.py:174
  975.0 56.7 %shard_map.158 = (bf16[4096,4096]{1,0:T(8,128)(2,1)}, f32[8,4096]{1,0:T(8,128)}) custom-call(s32[1]{0:T(128)} %bitcast.c_ref, bf16[4096,1024]{1,0:T(8,128)(2,1)} %yl_ref.7, bf16[2048,1024]{1,0:T(8,128)(2,1)} %collective-permute-done.8.yr_ref, bf16[8192,1024]{1,0:T(8,128)(2,1)} %all-gather.9.cloned.1.call-done.wl_ref, ...), custom_call_target="tpu_custom_call", output_to_operand_aliasing={{0}: (6, {})} | custom-call | flops 34359738368 | bytes 58720256 | tf_op jit(solution)/shard_map/pallas_call | solution.py:174
  1031.7 43.6 %fusion.12 = f32[4096,1024]{1,0:T(8,128)} fusion(bf16[4096,4096]{1,0:T(8,128)(2,1)} %get-tuple-element.117, bf16[2048,4096]{1,0:T(8,128)(2,1)} %all-gather.7.cloned.1.call-done.w_ref, s32[]{:T(128)S(6)} %select_n.29), kind=kOutput, calls=%fused_computation.18 | convolution fusion | flops 34359738368 | bytes 58720260 | tf_op jit(solution)/shard_map/dot_general | solution.py:32
  1075.3 48.4 %fusion.11 = (f32[1024]{0:T(1024)S(1)}, f32[4096]{0:T(1024)S(1)}, f32[4096]{0:T(1024)S(1)}, f32[1024]{0:T(1024)S(1)}, f32[4096,1024]{1,0:T(8,128)}) fusion(bf16[4096,1024]{1,0:T(8,128)(2,1)} %xl_ref.7, f32[4096]{0:T(1024)S(1)} %get-tuple-element.127, f32[4096]{0:T(1024)S(1)} %get-tuple-element.126, f32[1024]{0:T(1024)S(1)} %copy-done.11, ...), kind=kOutput, calls=%fused_computation.13 | convolution fusion | flops 34405867520 | bytes 83963904 | tf_op jit(solution)/shard_map/dot_general | solution.py:32
  1123.8 11.2 psum.15
  1135.0 0.6 slice.75
  1135.6 8.0 psum.14
  1143.6 0.6 fusion.19
  1144.3 15.8 %fusion.10 = bf16[4096,1024]{1,0:T(8,128)(2,1)} fusion(bf16[4096,1024]{1,0:T(8,128)(2,1)} %xl_ref.7, bf16[4096,1024]{1,0:T(8,128)(2,1)} %yl_ref.7, f32[4096,1024]{1,0:T(8,128)} %get-tuple-element.145, f32[4096]{0:T(1024)S(1)} %bitcast.34, f32[4096]{0:T(1024)S(1)} %bitcast.33, f32[4096]{0:T(1024)S(1)} %get-tuple-element.127, f32[1024]{0:T(1024)S(1)} %copy-done.11, ...), kind=kLoop, calls=%fused_computation.12 | loop fusion | flops 46137344 | bytes 42012672 | tf_op jit(solution)/shard_map/convert_element_type | solution.py:284
  1160.0 6.1 convert_element_type.39
  1166.1 6.0 convert_element_type.36
  (51 shorter events, 0.3 us)
Async XLA Ops:
  7.2 213.2 %all-gather.5.cloned.1.call-start = ((), (), s32[]{:S(2)}) async-start(), calls=%async_computation.2 | async-start | bytes 20971520 | tf_op jit(solution)/shard_map/all_gather | solution.py:202
  7.9 275.0 %all-gather.7.cloned.1.call-start = ((), (), s32[]{:S(2)}) async-start(), calls=%async_computation.3 | async-start | bytes 20971520 | tf_op jit(solution)/shard_map/all_gather | solution.py:202
  7.9 94.2 %collective-permute-start.7 = (bf16[512,4096]{1,0:T(8,128)(2,1)}, bf16[512,4096]{1,0:T(8,128)(2,1)}, u32[]{:S(2)}, u32[]{:S(2)}) collective-permute-start(bf16[512,4096]{1,0:T(8,128)(2,1)} %param.11), channel_id=1, source_target_pairs={{0,4},{4,0},{1,5},{5,1},{2,6},{6,2},{3,7},{7,3}} | collective-permute-start | bytes 12582920 | tf_op jit(solution)/shard_map/ppermute | solution.py:199
  102.2 487.6 %all-gather.9.cloned.1.call-start = ((), (), s32[]{:S(2)}) async-start(), calls=%async_computation.4 | async-start | bytes 20971520 | tf_op jit(solution)/shard_map/all_gather | solution.py:202
  103.0 14.8 %copy-start.14 = (bf16[4096]{0:T(1024)(128)(2,1)S(1)}, bf16[4096]{0:T(1024)(128)(2,1)}, u32[]{:S(2)}) copy-start(bf16[4096]{0:T(1024)(128)(2,1)} %param.12) | copy-start | bytes 24580
  103.0 14.8 %copy-start.10 = (f32[1024]{0:T(1024)S(1)}, f32[1024]{0:T(1024)}, u32[]{:S(2)}) copy-start(f32[1024]{0:T(1024)} %param.9) | copy-start | bytes 12292
  103.0 14.7 %copy-start.13 = (f32[1024]{0:T(1024)S(1)}, f32[1024]{0:T(1024)}, u32[]{:S(2)}) copy-start(f32[1024]{0:T(1024)} %param.10) | copy-start | bytes 12292
  103.0 580.7 %all-gather.11.cloned.1.call-start = ((), (), s32[]{:S(2)}) async-start(), calls=%async_computation.5 | async-start | bytes 20971520 | tf_op jit(solution)/shard_map/all_gather | solution.py:202
  103.0 8.9 copy-start
  115.7 97.1 %collective-permute-start.5 = (bf16[1024,1024]{1,0:T(8,128)(2,1)}, bf16[1024,1024]{1,0:T(8,128)(2,1)S(1)}, u32[]{:S(2)}, u32[]{:S(2)}) collective-permute-start(bf16[1024,1024]{1,0:T(8,128)(2,1)} %get-tuple-element.69), channel_id=1, source_target_pairs={{0,4},{4,0},{1,5},{5,1},{2,6},{6,2},{3,7},{7,3}} | collective-permute-start | bytes 6291464 | tf_op jit(solution)/shard_map/ppermute | solution.py:199
  117.4 131.0 %collective-permute-start.4 = (bf16[1024,1024]{1,0:T(8,128)(2,1)}, bf16[1024,1024]{1,0:T(8,128)(2,1)}, u32[]{:S(2)}, u32[]{:S(2)}) collective-permute-start(bf16[1024,1024]{1,0:T(8,128)(2,1)} %get-tuple-element.68), channel_id=1, source_target_pairs={{0,4},{4,0},{1,5},{5,1},{2,6},{6,2},{3,7},{7,3}} | collective-permute-start | bytes 6291464 | tf_op jit(solution)/shard_map/ppermute | solution.py:199
  117.7 102.7 %copy-start.6 = (f32[4096]{0:T(1024)}, f32[4096]{0:T(1024)S(1)}, u32[]{:S(2)}) copy-start(f32[4096]{0:T(1024)S(1)} %convert_element_type.31) | copy-start | bytes 49156
  117.7 92.1 %collective-permute-start.6 = (f32[6144]{0:T(1024)S(1)}, f32[6144]{0:T(1024)S(1)}, u32[]{:S(2)}, u32[]{:S(2)}) collective-permute-start(f32[6144]{0:T(1024)S(1)} %pad_maximum_fusion.2), channel_id=1, source_target_pairs={{0,4},{4,0},{1,5},{5,1},{2,6},{6,2},{3,7},{7,3}} | collective-permute-start | bytes 73736 | tf_op jit(solution)/shard_map/ppermute | solution.py:199
  119.4 377.6 %collective-permute-start.1 = (bf16[2048,1024]{1,0:T(8,128)(2,1)}, bf16[2048,1024]{1,0:T(8,128)(2,1)}, u32[]{:S(2)}, u32[]{:S(2)}) collective-permute-start(bf16[2048,1024]{1,0:T(8,128)(2,1)} %param.13), channel_id=1, source_target_pairs={{0,4},{4,0},{1,5},{5,1},{2,6},{6,2},{3,7},{7,3}} | collective-permute-start | bytes 12582920 | tf_op jit(solution)/shard_map/ppermute | solution.py:199
  119.8 225.0 %collective-permute-start.3 = (bf16[1024,1024]{1,0:T(8,128)(2,1)}, bf16[1024,1024]{1,0:T(8,128)(2,1)}, u32[]{:S(2)}, u32[]{:S(2)}) collective-permute-start(bf16[1024,1024]{1,0:T(8,128)(2,1)} %get-tuple-element.67), channel_id=1, source_target_pairs={{0,4},{4,0},{1,5},{5,1},{2,6},{6,2},{3,7},{7,3}} | collective-permute-start | bytes 6291464 | tf_op jit(solution)/shard_map/ppermute | solution.py:199
  209.9 197.4 %collective-permute-start.2 = (bf16[1024,1024]{1,0:T(8,128)(2,1)}, bf16[1024,1024]{1,0:T(8,128)(2,1)}, u32[]{:S(2)}, u32[]{:S(2)}) collective-permute-start(bf16[1024,1024]{1,0:T(8,128)(2,1)} %get-tuple-element.66), channel_id=1, source_target_pairs={{0,4},{4,0},{1,5},{5,1},{2,6},{6,2},{3,7},{7,3}} | collective-permute-start | bytes 6291464 | tf_op jit(solution)/shard_map/ppermute | solution.py:199
  212.8 1.4 copy-start.1
  497.1 662.9 %reduce-scatter.5.cloned.1.call-start = ((), (), s32[]{:S(2)}) async-start(), calls=%async_computation.7 | async-start | bytes 41943040 | tf_op jit(solution)/shard_map/reduce_scatter | solution.py:251
  589.8 2.1 copy-start.15
  589.9 576.2 %reduce-scatter.3.cloned.1.call-start = ((), (), s32[]{:S(2)}) async-start(), calls=%async_computation.6 | async-start | bytes 41943040 | tf_op jit(solution)/shard_map/reduce_scatter | solution.py:268
  589.9 93.8 %collective-permute-start = (bf16[2048,1024]{1,0:T(8,128)(2,1)}, bf16[2048,1024]{1,0:T(8,128)(2,1)}, u32[]{:S(2)}, u32[]{:S(2)}) collective-permute-start(bf16[2048,1024]{1,0:T(8,128)(2,1)} %get-tuple-element.65), channel_id=1, source_target_pairs={{0,4},{4,0},{1,5},{5,1},{2,6},{6,2},{3,7},{7,3}} | collective-permute-start | bytes 12582920 | tf_op jit(solution)/shard_map/ppermute | solution.py:199
  591.8 178.0 %collective-permute-start.8 = (bf16[2048,1024]{1,0:T(8,128)(2,1)}, bf16[2048,1024]{1,0:T(8,128)(2,1)}, u32[]{:S(2)}, u32[]{:S(2)}) collective-permute-start(bf16[2048,1024]{1,0:T(8,128)(2,1)} %get-tuple-element.109), channel_id=1, source_target_pairs={{0,4},{4,0},{1,5},{5,1},{2,6},{6,2},{3,7},{7,3}} | collective-permute-start | bytes 12582920 | tf_op jit(solution)/shard_map/ppermute | solution.py:199
  905.7 6.3 copy-start.2
  905.7 6.4 copy-start.3
  905.7 6.4 copy-start.4
  905.7 6.5 copy-start.5
  905.8 8.2 copy-start.7
  905.8 8.2 copy-start.8
  1031.7 43.6 %copy-start.11 = (f32[1024]{0:T(1024)S(1)}, f32[1024]{0:T(1024)}, u32[]{:S(2)}) copy-start(f32[1024]{0:T(1024)} %param.9) | copy-start | bytes 12292
  1075.3 48.5 %copy-start.9 = (f32[4096]{0:T(1024)S(1)}, f32[4096]{0:T(1024)}, u32[]{:S(2)}) copy-start(f32[4096]{0:T(1024)} %add_reduce_fusion) | copy-start | bytes 49156
  1075.3 48.5 %copy-start.12 = (f32[1024]{0:T(1024)S(1)}, f32[1024]{0:T(1024)}, u32[]{:S(2)}) copy-start(f32[1024]{0:T(1024)} %add.42) | copy-start | bytes 12292
Sparse Core Ops, SparseCore 0:
  9.5 105.9 all-gather.4
  117.0 103.1 all-gather.6
  221.6 103.1 all-gather.8
  497.2 104.2 all-gather.10
  603.9 226.7 reduce-scatter.4
  905.9 227.6 reduce-scatter.2

commit v2 on v1

v2 whole, which is shorter than its diff:
```python
import functools

import jax
import jax.numpy as jnp
from jax import lax
from jax.experimental import pallas as pl
from jax.experimental.pallas import tpu as pltpu
from jax.sharding import PartitionSpec as P


LN_EPS = 1e-5
GELU_K = 0.7978845608028654
GELU_A = 0.044715
CONTRACT_ROWS = (((0,), (0,)), ((), ()))
CONTRACT_COLS = (((1,), (1,)), ((), ()))
CONTRACT_MM = (((1,), (0,)), ((), ()))
XCUTS = (0, 1, 2, 4)
SUB = 256
VMEM = 58 * 1024 * 1024


def gelu_pair(u_val):
    sq = u_val * u_val
    half = 0.5 + 0.5 * jnp.tanh(u_val * (GELU_K + (GELU_K * GELU_A) * sq))
    act = u_val * half
    return act, half + (act * (1.0 - half)) * (2.0 * GELU_K + (6.0 * GELU_K * GELU_A) * sq)


def dot32(a, b, dims=CONTRACT_MM):
    return lax.dot_general(a, b, dims, preferred_element_type=jnp.float32)


def ln_kernel(c_ref, xl_ref, xr_ref, g_ref, b_ref, *refs):
    z_ref, st_ref = refs[-2:]
    width = xl_ref.shape[1]
    first = c_ref[0] == 0
    xl = xl_ref[...].astype(jnp.float32)
    xr = xr_ref[...].astype(jnp.float32)
    total = jnp.sum(xl, axis=1, keepdims=True) + jnp.sum(xr, axis=1, keepdims=True)
    square = jnp.sum(xl * xl, axis=1, keepdims=True) + jnp.sum(xr * xr, axis=1, keepdims=True)
    mean = total / (2 * width)
    inv = lax.rsqrt(square / (2 * width) - mean * mean + LN_EPS)
    hl = (xl - mean) * inv
    hr = (xr - mean) * inv
    lo = jnp.where(first, hl, hr)
    hi = jnp.where(first, hr, hl)
    z_ref[:, :width] = (lo * g_ref[:, :width] + b_ref[:, :width]).astype(z_ref.dtype)
    z_ref[:, width:] = (hi * g_ref[:, width:] + b_ref[:, width:]).astype(z_ref.dtype)
    lane = lax.broadcasted_iota(jnp.int32, st_ref.shape, 1)
    st_ref[...] = jnp.where(lane == 0, mean, inv)


def ln_call(cvec, x_in, x_rem, gain, bias, start, z_buf):
    rows, width = x_rem.shape
    tokens = x_in.shape[0]
    bm = 256
    off = start // bm
    in_specs = [
        pl.BlockSpec((bm, width), lambda i, c: (off + i, 0)),
        pl.BlockSpec((bm, width), lambda i, c: (i, 0)),
        pl.BlockSpec((1, 2 * width), lambda i, c: (0, 0)),
        pl.BlockSpec((1, 2 * width), lambda i, c: (0, 0)),
    ]
    args = [cvec, x_in, x_rem, gain, bias]
    alias = {}
    if z_buf is not None:
        in_specs.append(pl.BlockSpec(memory_space=pl.ANY))
        args.append(z_buf)
        alias = {5: 0}
    return pl.pallas_call(
        ln_kernel,
        grid_spec=pltpu.PrefetchScalarGridSpec(
            num_scalar_prefetch=1,
            grid=(rows // bm,),
            in_specs=in_specs,
            out_specs=[
                pl.BlockSpec((bm, 2 * width), lambda i, c: (off + i, 0)),
                pl.BlockSpec((bm, 128), lambda i, c: (i, 0)),
            ],
        ),
        out_shape=[
            jax.ShapeDtypeStruct((tokens, 2 * width), jnp.bfloat16),
            jax.ShapeDtypeStruct((rows, 128), jnp.float32),
        ],
        input_output_aliases=alias,
        compiler_params=pltpu.CompilerParams(vmem_limit_bytes=VMEM),
        cost_estimate=pl.CostEstimate(flops=rows * width * 400, bytes_accessed=rows * width * 8, transcendentals=0),
    )(*args)


def ua_kernel(c_ref, z_ref, w_ref, b_ref, *refs):
    g_ref, a_ref = refs[-2:]
    for i in range(z_ref.shape[0] // SUB):
        part = pl.ds(i * SUB, SUB)
        u = (dot32(z_ref[part, :], w_ref[...]) + b_ref[...]).astype(a_ref.dtype)
        act, grad = gelu_pair(u.astype(jnp.float32))
        a_ref[part, :] = act.astype(a_ref.dtype)
        g_ref[part, :] = grad


def ua_call(cvec, z_buf, w_half, b_half, start, rows, other, bufs):
    tokens, width = z_buf.shape
    ffh = w_half.shape[1]
    k = start // rows
    bn = 512
    nb = ffh // bn

    def col(j, c):
        return ((1 - c[0]) if other else c[0]) * nb + j

    in_specs = [
        pl.BlockSpec((rows, width), lambda j, c: (k, 0)),
        pl.BlockSpec((width, bn), lambda j, c: (0, j)),
        pl.BlockSpec((1, bn), lambda j, c: (0, j)),
    ]
    args = [cvec, z_buf, w_half, b_half]
    alias = {}
    if bufs is not None:
        in_specs += [pl.BlockSpec(memory_space=pl.ANY)] * 2
        args += list(bufs)
        alias = {4: 0, 5: 1}
    out = pl.BlockSpec((rows, bn), lambda j, c: (k, col(j, c)))
    return pl.pallas_call(
        ua_kernel,
        grid_spec=pltpu.PrefetchScalarGridSpec(
            num_scalar_prefetch=1, grid=(nb,), in_specs=in_specs, out_specs=[out, out]),
        out_shape=[
            jax.ShapeDtypeStruct((tokens, 2 * ffh), jnp.float32),
            jax.ShapeDtypeStruct((tokens, 2 * ffh), jnp.bfloat16),
        ],
        input_output_aliases=alias,
        compiler_params=pltpu.CompilerParams(vmem_limit_bytes=VMEM),
        cost_estimate=pl.CostEstimate(
            flops=2 * rows * width * ffh, bytes_accessed=2 * (rows * width + width * ffh + 3 * rows * ffh),
            transcendentals=rows * ffh),
    )(*args)


def du_kernel(with_sum, c_ref, yl_ref, yr_ref, wl_ref, wr_ref, g_ref, du_ref, *refs):
    total = 0.0
    for i in range(yl_ref.shape[0] // SUB):
        part = pl.ds(i * SUB, SUB)
        da = dot32(yl_ref[part, :], wl_ref[...], CONTRACT_COLS) + dot32(yr_ref[part, :], wr_ref[...], CONTRACT_COLS)
        du = (da * g_ref[part, :]).astype(du_ref.dtype)
        du_ref[part, :] = du
        if with_sum:
            total += jnp.sum(du.astype(jnp.float32).reshape(SUB // 8, 8, -1), axis=0)
    if with_sum:
        refs[0][...] = total


def du_call(cvec, dy_out, dy_rem, w_own, w_oth, g_buf, other):
    tokens, dloc = dy_out.shape
    ffh = w_own.shape[0] // 2
    rows = tokens // 2
    bn = 512
    nb = ffh // bn

    def off(j, c):
        return ((1 - c[0]) if other else c[0]) * nb + j

    in_specs = [
        pl.BlockSpec((rows, dloc), lambda i, j, c: (i, 0)),
        pl.BlockSpec((rows, dloc), lambda i, j, c: (i, 0)),
        pl.BlockSpec((bn, dloc), lambda i, j, c: (off(j, c), 0)),
        pl.BlockSpec((bn, dloc), lambda i, j, c: (off(j, c), 0)),
        pl.BlockSpec((rows, bn), lambda i, j, c: (i, off(j, c))),
    ]
    out_specs = [pl.BlockSpec((rows, bn), lambda i, j, c: (i, j))]
    out_shape = [jax.ShapeDtypeStruct((tokens, ffh), jnp.bfloat16)]
    if not other:
        out_specs.append(pl.BlockSpec((8, bn), lambda i, j, c: (i, j)))
        out_shape.append(jax.ShapeDtypeStruct((8 * (tokens // rows), ffh), jnp.float32))
    return pl.pallas_call(
        functools.partial(du_kernel, not other),
        grid_spec=pltpu.PrefetchScalarGridSpec(
            num_scalar_prefetch=1, grid=(tokens // rows, nb), in_specs=in_specs, out_specs=out_specs),
        out_shape=out_shape,
        compiler_params=pltpu.CompilerParams(vmem_limit_bytes=VMEM),
        cost_estimate=pl.CostEstimate(
            flops=4 * tokens * dloc * ffh, bytes_accessed=4 * (tokens * dloc + dloc * ffh + 2 * tokens * ffh),
            transcendentals=0),
    )(cvec, dy_out, dy_rem, w_own, w_oth, g_buf)


def solution(mesh):
    swap = [(0, 1), (1, 0)]
    core_swap = [(0, 1), (1, 0), (2, 3), (3, 2)]
    x_swap = [(0, 2), (2, 0), (1, 3), (3, 1)]
    barrier = lax.optimization_barrier

    def swap_col(v):
        return lax.ppermute(v, 'col', swap)

    def gather_row(v):
        return lax.all_gather(v, 'row', axis=0, tiled=True)

    def local_step(x_in, ln_gain, ln_bias, w_up, b_up, w_down, b_down, dy_out):
        cid = lax.axis_index('col')
        cvec = jnp.full((1,), cid, jnp.int32)
        first = cid == 0
        tokens, dloc = x_in.shape
        width = dloc * mesh.shape['col']
        ffh = w_up.shape[1]
        cuts = [c * tokens // XCUTS[-1] for c in XCUTS]
        pieces = barrier([x_in[a:b] for a, b in zip(cuts, cuts[1:])] + [dy_out])
        vecs = jnp.concatenate([ln_gain, ln_bias, b_up.astype(jnp.float32)])
        vecs_o = swap_col(vecs)
        w_up_sw = swap_col(w_up)
        x_o = [swap_col(v) for v in pieces[:-1]]
        w_dn_sw = swap_col(w_down)
        dy_o = swap_col(pieces[-1])
        w1_own = gather_row(w_up)
        w1_oth = gather_row(w_up_sw)
        w2_own = gather_row(w_down)
        db_loc = barrier(jnp.sum(pieces[-1].astype(jnp.float32), axis=0))

        def true_cols(own, oth):
            return jnp.concatenate([jnp.where(first, own, oth), jnp.where(first, oth, own)], axis=-1)[None]

        gain = true_cols(vecs[:dloc], vecs_o[:dloc])
        bias = true_cols(vecs[dloc:2 * dloc], vecs_o[dloc:2 * dloc])
        w1 = (w1_own, w1_oth)
        b1 = (vecs[None, 2 * dloc:], vecs_o[None, 2 * dloc:])

        z_buf, bufs, stats = None, None, []
        todo = (((0, 1024, 0),), ((1024, 1024, 0), (0, 2048, 1)), ((2048, 2048, 0), (2048, 2048, 1)))
        for k, calls in enumerate(todo):
            if bufs is not None:
                x_o[k], bufs, z_buf = barrier((x_o[k], bufs, z_buf))
            z_buf, st = ln_call(cvec, x_in, x_o[k], gain, bias, cuts[k], z_buf)
            stats.append(st)
            for start, rows, other in calls:
                bufs = ua_call(cvec, z_buf, w1[other], b1[other], start, rows, other, bufs)
        w_dn_sw, bufs = barrier((w_dn_sw, bufs))
        g_buf, a_buf = bufs
        w2_oth = gather_row(w_dn_sw)

        dw2 = dot32(a_buf, dy_out, CONTRACT_ROWS)
        w2_own, dw2 = barrier((w2_own, dw2))
        dw_down = lax.psum_scatter(dw2, 'row', scatter_dimension=0, tiled=True).astype(jnp.bfloat16)
        x_f32 = x_in.astype(jnp.float32)
        y_sum = dot32(a_buf, w2_own)
        y_out = (x_f32 + y_sum + b_down.astype(jnp.float32)).astype(jnp.bfloat16)
        dy_o, y_out = barrier((dy_o, y_out))

        du_own, sum_own = du_call(cvec, dy_out, dy_o, w2_own, w2_oth, g_buf, 0)
        db_up = jnp.sum(sum_own, axis=0)
        n_sc = ffh * 3 // 4
        dwu = dot32(z_buf, du_own[:, :n_sc], CONTRACT_ROWS)
        du_own, dwu = barrier((du_own, dwu))
        dw_left = lax.psum_scatter(dwu, 'row', scatter_dimension=0, tiled=True).astype(jnp.bfloat16)
        rid = lax.axis_index('row')
        xid, core = rid // 2, rid % 2
        blk = dloc * mesh.shape['col'] // mesh.shape['row']

        dwu_b = dot32(z_buf, du_own[:, n_sc:], CONTRACT_ROWS)

        def dwu_rows(xi, ci):
            return lax.dynamic_slice_in_dim(dwu_b, (2 * xi + ci) * blk, blk, 0)

        got_o = lax.ppermute(dwu_rows(1 - xid, 1 - core), 'row', core_swap)
        got_s = lax.ppermute(dwu_rows(xid, 1 - core), 'row', core_swap)
        got_x = lax.ppermute(dwu_rows(1 - xid, core) + got_o, 'row', x_swap)
        keep_x = dwu_rows(xid, core) + got_s
        dwu_b, g_buf, du_own = barrier((dwu_b, g_buf, du_own))
        du_oth = du_call(cvec, dy_out, dy_o, w2_own, w2_oth, g_buf, 1)[0]

        w1_own_r = lax.dynamic_slice_in_dim(w1_own, cid * dloc, dloc, 0)
        w1_oth_r = lax.dynamic_slice_in_dim(w1_oth, cid * dloc, dloc, 0)
        dz = dot32(du_own, w1_own_r, CONTRACT_COLS) + dot32(du_oth, w1_oth_r, CONTRACT_COLS)

        st = jnp.concatenate(stats, axis=0)
        mean_x, inv_std = st[:, 0:1], st[:, 1:2]
        x_hat = (x_f32 - mean_x) * inv_std
        value_a6 = dz * ln_gain
        row_sums = jnp.concatenate([jnp.sum(value_a6, axis=1, keepdims=True), jnp.sum(value_a6 * x_hat, axis=1, keepdims=True)], axis=1)
        row_sums = row_sums + lax.ppermute(row_sums, 'col', swap)
        sums = jnp.concatenate([db_up, db_loc, jnp.sum(dz * x_hat, axis=0), jnp.sum(dz, axis=0)])
        sums = sums + lax.ppermute(sums, 'row', core_swap)
        sums = sums + lax.ppermute(sums, 'row', x_swap)
        mean_dxh = row_sums[:, 0:1] / width
        mean_dxh_xh = row_sums[:, 1:2] / width
        dx_in = (dy_out.astype(jnp.float32) + inv_std * (value_a6 - mean_dxh - x_hat * mean_dxh_xh)).astype(jnp.bfloat16)
        dw_up = jnp.concatenate([dw_left, (keep_x + got_x).astype(jnp.bfloat16)], axis=1)
        db_up, db_down, d_gain, d_bias = sums[:ffh], sums[ffh:ffh + dloc], sums[ffh + dloc:ffh + 2 * dloc], sums[ffh + 2 * dloc:]
        return (y_out, dx_in, dw_up, db_up, dw_down, db_down, d_gain, d_bias)

    blk_spec = P('row', 'col')
    vec_spec = P('col')
    return jax.shard_map(local_step, mesh=mesh, in_specs=(blk_spec, vec_spec, vec_spec, blk_spec, vec_spec, blk_spec, vec_spec, blk_spec), out_specs=(blk_spec, blk_spec, blk_spec, vec_spec, blk_spec, vec_spec, vec_spec, vec_spec), check_vma=False)
```

time: 1190 us -> 1230 us (1.034)
  waiting for transfers between devices: 255 us -> 354 us
  Pallas kernels: 479 us -> 430 us
  blocking collectives: 19.2 us -> 0 us
    ppermute x9 -> x7, waiting for transfers between devices: 254 us -> 320 us  [swap_col(): return lax.ppermute(v, 'col', swap)]
    pallas_call x4 -> x2, Pallas kernels: 230 us -> 166 us  [du_call(): pl.pallas_call(functools.partial(du_kernel, not other), grid_spec=pltpu.P...]
    ppermute x0 -> x6, waiting for transfers between devices: none -> 32.5 us  [the longest x1 29.9 us: local_step(): got_x = lax.ppermute(dwu_rows(1 - xid, core) + got_o, 'row', x_swap)]
    psum x2 -> x0, blocking collectives: 19.2 us -> none  [the longest x1 11.2 us: local_step(): lax.psum(jnp.concatenate([db_up, db_loc, jnp.sum(dz * x_hat, axis=0), jnp...]
    pallas_call x8 -> x5, Pallas kernels: 224 us -> 239 us  [ua_call(): pl.pallas_call(ua_kernel, grid_spec=pltpu.PrefetchScalarGridSpec(num_scal...]
    pallas_call x4 -> x3, Pallas kernels: 25.3 us -> 24.3 us  [ln_call(): pl.pallas_call(ln_kernel, grid_spec=pltpu.PrefetchScalarGridSpec(num_scal...]
    dot_general x5 -> x6, matrix products: 344 us -> 343 us  [dot32(): return lax.dot_general(a, b, dims, preferred_element_type=jnp.float32)]
  transfers between devices with their start and end apart: 15 -> 19, of which waited for: 5 -> 6; matrix products, arithmetic and copies ran while one was open for 33% -> 33% of each run, Pallas kernels for 41% -> 35%
where the time goes in v2:
time: 1230 us; the launch traced here: 1220 us
  Pallas kernels  430 us (35%)
  waiting for transfers between devices  354 us (29%)
  matrix products  343 us (28%)
  other arithmetic  39.4 us (3%)
  local copies, waits for them, and re-layouts  29.2 us (2%)
  between operations  14.6 us (1%)
  starting transfers between devices  12.5 us (1%)
    dot_general x6, matrix products, dot32(): return lax.dot_general(a, b, dims, preferred_element_type=jnp.float32)  343 us
    ppermute x7, waiting for transfers between devices, swap_col(): return lax.ppermute(v, 'col', swap)  320 us
    pallas_call x5, Pallas kernels, ua_call(): pl.pallas_call(ua_kernel, grid_spec=pltpu.PrefetchScalarGridSpec(num_scal...  239 us
    pallas_call x2, Pallas kernels, du_call(): pl.pallas_call(functools.partial(du_kernel, not other), grid_spec=pltpu.P...  166 us
    ppermute x1, waiting for transfers between devices, local_step(): got_x = lax.ppermute(dwu_rows(1 - xid, core) + got_o, 'row', x_swap)  29.9 us
  transfers between devices with their start and end apart: 19, of which 6 were waited for; matrix products, arithmetic and copies ran while one was open for 33% of the time, Pallas kernels for 35%

profile of v2, /device:TPU:0, one launch (start us, length us, event | category | flops | bytes accessed | tf_op | source)
XLA Modules:
  0.0 1223.0 jit_solution(12475736744716617856)
XLA Ops:
  7.2 0.0 all-gather.5.cloned.1.call-start
  7.2 0.7 all-gather.5.cloned.1.call-update
  7.9 0.0 all-gather.7.cloned.1.call-start
  8.0 3.4 collective-permute-start.6
  11.3 90.9 %collective-permute-done.6 = bf16[512,4096]{1,0:T(8,128)(2,1)} collective-permute-done((bf16[512,4096]{1,0:T(8,128)(2,1)}, bf16[512,4096]{1,0:T(8,128)(2,1)}, u32[]{:S(2)}, u32[]{:S(2)}) %collective-permute-start.6) | collective-permute-done | bytes 4194336 | tf_op jit(solution)/shard_map/ppermute | solution.py:193
  102.2 0.0 all-gather.9.cloned.1.call-start
  102.3 0.7 all-gather.9.cloned.1.call-update
  103.0 0.0 all-gather.11.cloned.1.call-start
  103.0 4.8 slice.50
  107.8 4.0 fusion.23
  111.8 1.7 collective-permute-start.4
  113.5 0.4 collective-permute-start.3
  113.8 1.7 collective-permute-start.5
  115.5 0.4 collective-permute-start.1
  115.9 1.7 collective-permute-start.2
  117.6 88.4 %collective-permute-done.5 = f32[6144]{0:T(1024)S(1)} collective-permute-done((f32[6144]{0:T(1024)S(1)}, f32[6144]{0:T(1024)S(1)}, u32[]{:S(2)}, u32[]{:S(2)}) %collective-permute-start.5) | collective-permute-done | bytes 24608 | tf_op jit(solution)/shard_map/ppermute | solution.py:193
  206.0 0.6 slice.66
  206.6 0.6 pad_maximum_fusion.4
  207.2 6.3 shard_map.143
  213.5 31.3 %shard_map.144 = (f32[4096,8192]{1,0:T(8,128)}, bf16[4096,8192]{1,0:T(8,128)(2,1)}) custom-call(s32[1]{0:T(128)} %bitcast.c_ref, bf16[4096,2048]{1,0:T(8,128)(2,1)} %get-tuple-element.57.z_ref.refs_0_, bf16[2048,4096]{1,0:T(8,128)(2,1)} %all-gather.5.cloned.1.call-done.w_ref, f32[1,4096]{1,0:T(1,128)} %bitcast.18), custom_call_target="tpu_custom_call" | custom-call | flops 17179869184 | bytes 46137344 | tf_op jit(solution)/shard_map/pallas_call | solution.py:123
  244.8 6.5 shard_map.145
  251.3 31.3 %shard_map.146 = (f32[4096,8192]{1,0:T(8,128)}, bf16[4096,8192]{1,0:T(8,128)(2,1)}) custom-call(s32[1]{0:T(128)} %bitcast.c_ref, bf16[4096,2048]{1,0:T(8,128)(2,1)} %get-tuple-element.66.z_ref.refs_0_, bf16[2048,4096]{1,0:T(8,128)(2,1)} %all-gather.5.cloned.1.call-done.w_ref, f32[1,4096]{1,0:T(1,128)} %bitcast.19, ...), custom_call_target="tpu_custom_call", output_to_operand_aliasing={{0}: (4, {}), {1}: (5, {})} | custom-call | flops 17179869184 | bytes 46137344 | tf_op jit(solution)/shard_map/pallas_call | solution.py:123
  282.6 58.8 %shard_map.147 = (f32[4096,8192]{1,0:T(8,128)}, bf16[4096,8192]{1,0:T(8,128)(2,1)}) custom-call(s32[1]{0:T(128)} %bitcast.c_ref, bf16[4096,2048]{1,0:T(8,128)(2,1)} %get-tuple-element.66.z_ref.refs_0_, bf16[2048,4096]{1,0:T(8,128)(2,1)} %all-gather.7.cloned.1.call-done.w_ref, f32[1,4096]{1,0:T(1,128)} %bitcast.21, ...), custom_call_target="tpu_custom_call", output_to_operand_aliasing={{0}: (4, {}), {1}: (5, {})} | custom-call | flops 34359738368 | bytes 75497472 | tf_op jit(solution)/shard_map/pallas_call | solution.py:123
  341.4 42.7 %collective-permute-done.2.xr_ref = bf16[2048,1024]{1,0:T(8,128)(2,1)} collective-permute-done((bf16[2048,1024]{1,0:T(8,128)(2,1)}, bf16[2048,1024]{1,0:T(8,128)(2,1)}, u32[]{:S(2)}, u32[]{:S(2)}) %collective-permute-start.2) | collective-permute-done | bytes 4194336 | tf_op jit(solution)/shard_map/ppermute | solution.py:193
  384.1 11.5 shard_map.148
  395.6 58.7 %shard_map.149 = (f32[4096,8192]{1,0:T(8,128)}, bf16[4096,8192]{1,0:T(8,128)(2,1)}) custom-call(s32[1]{0:T(128)} %bitcast.c_ref, bf16[4096,2048]{1,0:T(8,128)(2,1)} %get-tuple-element.67.z_ref, bf16[2048,4096]{1,0:T(8,128)(2,1)} %all-gather.5.cloned.1.call-done.w_ref, f32[1,4096]{1,0:T(1,128)} %bitcast.20, ...), custom_call_target="tpu_custom_call", output_to_operand_aliasing={{0}: (4, {}), {1}: (5, {})} | custom-call | flops 34359738368 | bytes 75497472 | tf_op jit(solution)/shard_map/pallas_call | solution.py:123
  454.4 58.8 %shard_map.150 = (f32[4096,8192]{1,0:T(8,128)}, bf16[4096,8192]{1,0:T(8,128)(2,1)}) custom-call(s32[1]{0:T(128)} %bitcast.c_ref, bf16[4096,2048]{1,0:T(8,128)(2,1)} %get-tuple-element.67.z_ref, bf16[2048,4096]{1,0:T(8,128)(2,1)} %all-gather.7.cloned.1.call-done.w_ref, f32[1,4096]{1,0:T(1,128)} %bitcast.22, ...), custom_call_target="tpu_custom_call", output_to_operand_aliasing={{0}: (4, {}), {1}: (5, {})} | custom-call | flops 34359738368 | bytes 75497472 | tf_op jit(solution)/shard_map/pallas_call | solution.py:123
  513.1 0.0 reduce-scatter.5.cloned.1.call-start
  513.2 80.7 %fusion.25 = f32[8192,1024]{1,0:T(8,128)} fusion(bf16[4096,8192]{1,0:T(8,128)(2,1)} %get-tuple-element.74, bf16[4096,1024]{1,0:T(8,128)(2,1)} %yl_ref.3), kind=kOutput, calls=%fused_computation.52 | convolution fusion | flops 68719476736 | bytes 109051904 | tf_op jit(solution)/shard_map/dot_general | solution.py:30
  593.9 0.0 reduce-scatter.3.cloned.1.call-start
  594.0 1.2 collective-permute-start
  595.2 80.4 %fusion.3 = bf16[4096,1024]{1,0:T(8,128)(2,1)} fusion(bf16[4096,1024]{1,0:T(8,128)(2,1)} %xl_ref.5, bf16[4096,8192]{1,0:T(8,128)(2,1)} %get-tuple-element.74, bf16[8192,1024]{1,0:T(8,128)(2,1)} %all-gather.9.cloned.1.call-done.wl_ref, f32[1024]{0:T(1024)S(1)} %convert_element_type.32), kind=kOutput, calls=%fused_computation.5 | convolution fusion | flops 68736253952 | bytes 100667392 | tf_op jit(solution)/shard_map/dot_general | solution.py:30
  675.6 98.4 %collective-permute-done.yr_ref = bf16[4096,1024]{1,0:T(8,128)(2,1)} collective-permute-done((bf16[4096,1024]{1,0:T(8,128)(2,1)}, bf16[4096,1024]{1,0:T(8,128)(2,1)}, u32[]{:S(2)}, u32[]{:S(2)}) %collective-permute-start) | collective-permute-done | bytes 8388640 | tf_op jit(solution)/shard_map/ppermute | solution.py:193
  774.1 83.4 %shard_map.151 = (bf16[4096,4096]{1,0:T(8,128)(2,1)}, f32[16,4096]{1,0:T(8,128)}) custom-call(s32[1]{0:T(128)} %bitcast.c_ref, bf16[4096,1024]{1,0:T(8,128)(2,1)} %yl_ref.3, bf16[4096,1024]{1,0:T(8,128)(2,1)} %collective-permute-done.yr_ref, bf16[8192,1024]{1,0:T(8,128)(2,1)} %all-gather.9.cloned.1.call-done.wl_ref, ...), custom_call_target="tpu_custom_call" | custom-call | flops 68719476736 | bytes 167772160 | tf_op jit(solution)/shard_map/pallas_call | solution.py:174
  857.5 61.8 %fusion = f32[2048,3072]{1,0:T(8,128)} fusion(bf16[4096,2048]{1,0:T(8,128)(2,1)} %get-tuple-element.67.z_ref, bf16[4096,4096]{1,0:T(8,128)(2,1)} %get-tuple-element.85), kind=kOutput, calls=%fused_computation | convolution fusion | flops 51539607552 | bytes 67108864 | tf_op jit(solution)/shard_map/dot_general | solution.py:30
  919.4 5.8 convert_reduce_fusion
  925.3 0.1 constant_dynamic-update-slice_fusion
  925.4 2.3 slice_reduce_fusion.1
  927.7 27.9 %fusion.17 = f32[2048,1024]{0,1:T(8,128)} fusion(bf16[4096,2048]{1,0:T(8,128)(2,1)} %get-tuple-element.67.z_ref, bf16[4096,4096]{1,0:T(8,128)(2,1)} %get-tuple-element.85), kind=kOutput, calls=%fused_computation.22 | convolution fusion | flops 17179869184 | bytes 33554432 | tf_op jit(solution)/shard_map/dot_general | solution.py:30
  955.6 0.6 reduce_sum.56
  956.2 44.2 %fusion.15 = f32[4096,1024]{1,0:T(8,128)} fusion(bf16[4096,4096]{1,0:T(8,128)(2,1)} %get-tuple-element.85, bf16[2048,4096]{1,0:T(8,128)(2,1)} %all-gather.5.cloned.1.call-done.w_ref, s32[]{:T(128)S(6)} %select_n.52), kind=kOutput, calls=%fused_computation.20 | convolution fusion | flops 34359738368 | bytes 58720260 | tf_op jit(solution)/shard_map/dot_general | solution.py:30
  1000.4 83.0 %shard_map.152 = bf16[4096,4096]{1,0:T(8,128)(2,1)} custom-call(s32[1]{0:T(128)} %bitcast.c_ref, bf16[4096,1024]{1,0:T(8,128)(2,1)} %yl_ref.3, bf16[4096,1024]{1,0:T(8,128)(2,1)} %collective-permute-done.yr_ref, bf16[8192,1024]{1,0:T(8,128)(2,1)} %all-gather.9.cloned.1.call-done.wl_ref, bf16[8192,1024]{1,0:T(8,128)(2,1)} %all-gather.11.cloned.1.call-done.wr_ref, ...), custom_call_target="tpu_custom_call" | custom-call | flops 68719476736 | bytes 167772160 | tf_op jit(solution)/shard_map/pallas_call | solution.py:174
  1083.5 48.3 %fusion.13 = (f32[1024]{0:T(1024)S(1)}, f32[4096]{0:T(1024)S(1)}, f32[4096]{0:T(1024)S(1)}, f32[1024]{0:T(1024)S(1)}, f32[4096,1024]{1,0:T(8,128)}) fusion(bf16[4096,1024]{1,0:T(8,128)(2,1)} %xl_ref.5, f32[4096]{0:T(1024)S(1)} %copy-done.7, f32[4096]{0:T(1024)S(1)} %copy-done.6, f32[1024]{0:T(1024)S(1)} %copy-done.10, f32[4096,1024]{1,0:T(8,128)} %fusion.15, ...), kind=kOutput, calls=%fused_computation.15 | convolution fusion | flops 34405867520 | bytes 83963904 | tf_op jit(solution)/shard_map/dot_general | solution.py:30
  1131.8 0.0 collective-permute-start.11
  1131.9 6.6 constant_dynamic-slice_fusion.2
  1138.5 2.9 copy.37
  1141.3 0.5 collective-permute-start.9
  1141.8 2.9 copy.35
  1144.7 0.0 collective-permute-start.8
  1144.8 1.8 copy.36
  1146.6 1.9 copy.34
  1148.5 0.0 collective-permute-start.7
  1148.6 1.3 collective-permute-start.12
  1149.9 2.5 collective-permute-done.7
  1152.5 2.6 add.89
  1155.2 0.0 collective-permute-start.10
  1155.2 15.7 %fusion.12 = bf16[4096,1024]{1,0:T(8,128)(2,1)} fusion(bf16[4096,1024]{1,0:T(8,128)(2,1)} %xl_ref.5, bf16[4096,1024]{1,0:T(8,128)(2,1)} %yl_ref.3, f32[4096,1024]{1,0:T(8,128)} %get-tuple-element.113, f32[4096]{0:T(1024)S(1)} %bitcast.30, f32[4096]{0:T(1024)S(1)} %bitcast.29, f32[4096]{0:T(1024)S(1)} %copy-done.7, f32[1024]{0:T(1024)S(1)} %copy-done.10, ...), kind=kLoop, calls=%fused_computation.14 | loop fusion | flops 46137344 | bytes 42012672 | tf_op jit(solution)/shard_map/convert_element_type | solution.py:284
  1170.9 0.6 slice.71
  1171.5 0.6 fusion.24
  1172.1 29.9 %collective-permute-done.10 = f32[512,1024]{1,0:T(8,128)S(1)} collective-permute-done((f32[512,1024]{1,0:T(8,128)S(1)}, f32[512,1024]{1,0:T(8,128)S(1)}, u32[]{:S(2)}, u32[]{:S(2)}) %collective-permute-start.10) | collective-permute-done | bytes 2097184 | tf_op jit(solution)/shard_map/ppermute | solution.py:264
  1202.1 2.2 add_convert_fusion
  1204.3 6.1 convert_element_type.39
  1210.4 3.2 convert_element_type.36
  1213.6 2.4 pad_maximum_fusion
  (57 shorter events, 0.4 us)
Async XLA Ops:
  7.2 106.6 %copy-start.12 = (bf16[4096]{0:T(1024)(128)(2,1)S(1)}, bf16[4096]{0:T(1024)(128)(2,1)}, u32[]{:S(2)}) copy-start(bf16[4096]{0:T(1024)(128)(2,1)} %param.12) | copy-start | bytes 24580
  7.2 106.6 %copy-start.11 = (f32[1024]{0:T(1024)S(1)}, f32[1024]{0:T(1024)}, u32[]{:S(2)}) copy-start(f32[1024]{0:T(1024)} %param.10) | copy-start | bytes 12292
  7.2 106.6 %copy-start.9 = (f32[1024]{0:T(1024)S(1)}, f32[1024]{0:T(1024)}, u32[]{:S(2)}) copy-start(f32[1024]{0:T(1024)} %param.9) | copy-start | bytes 12292
  7.2 206.3 %all-gather.5.cloned.1.call-start = ((), (), s32[]{:S(2)}) async-start(), calls=%async_computation.2 | async-start | bytes 20971520 | tf_op jit(solution)/shard_map/all_gather | solution.py:196
  7.9 274.6 %all-gather.7.cloned.1.call-start = ((), (), s32[]{:S(2)}) async-start(), calls=%async_computation.3 | async-start | bytes 20971520 | tf_op jit(solution)/shard_map/all_gather | solution.py:196
  8.0 94.2 %collective-permute-start.6 = (bf16[512,4096]{1,0:T(8,128)(2,1)}, bf16[512,4096]{1,0:T(8,128)(2,1)}, u32[]{:S(2)}, u32[]{:S(2)}) collective-permute-start(bf16[512,4096]{1,0:T(8,128)(2,1)} %param.11), channel_id=1, source_target_pairs={{0,4},{4,0},{1,5},{5,1},{2,6},{6,2},{3,7},{7,3}} | collective-permute-start | bytes 12582920 | tf_op jit(solution)/shard_map/ppermute | solution.py:193
  102.2 491.7 %all-gather.9.cloned.1.call-start = ((), (), s32[]{:S(2)}) async-start(), calls=%async_computation.4 | async-start | bytes 20971520 | tf_op jit(solution)/shard_map/all_gather | solution.py:196
  103.0 671.1 %all-gather.11.cloned.1.call-start = ((), (), s32[]{:S(2)}) async-start(), calls=%async_computation.5 | async-start | bytes 20971520 | tf_op jit(solution)/shard_map/all_gather | solution.py:196
  111.8 95.4 %collective-permute-start.4 = (bf16[1024,1024]{1,0:T(8,128)(2,1)}, bf16[1024,1024]{1,0:T(8,128)(2,1)}, u32[]{:S(2)}, u32[]{:S(2)}) collective-permute-start(bf16[1024,1024]{1,0:T(8,128)(2,1)} %get-tuple-element.52), channel_id=1, source_target_pairs={{0,4},{4,0},{1,5},{5,1},{2,6},{6,2},{3,7},{7,3}} | collective-permute-start | bytes 6291464 | tf_op jit(solution)/shard_map/ppermute | solution.py:193
  113.5 131.3 %collective-permute-start.3 = (bf16[1024,1024]{1,0:T(8,128)(2,1)S(1)}, bf16[1024,1024]{1,0:T(8,128)(2,1)}, u32[]{:S(2)}, u32[]{:S(2)}) collective-permute-start(bf16[1024,1024]{1,0:T(8,128)(2,1)S(1)} %get-tuple-element.51), channel_id=1, source_target_pairs={{0,4},{4,0},{1,5},{5,1},{2,6},{6,2},{3,7},{7,3}} | collective-permute-start | bytes 6291464 | tf_op jit(solution)/shard_map/ppermute | solution.py:193
  113.8 99.7 %copy-start.3 = (f32[4096]{0:T(1024)}, f32[4096]{0:T(1024)S(1)}, u32[]{:S(2)}) copy-start(f32[4096]{0:T(1024)S(1)} %convert_element_type.31) | copy-start | bytes 49156
  113.8 92.1 %collective-permute-start.5 = (f32[6144]{0:T(1024)S(1)}, f32[6144]{0:T(1024)S(1)}, u32[]{:S(2)}, u32[]{:S(2)}) collective-permute-start(f32[6144]{0:T(1024)S(1)} %pad_maximum_fusion.3), channel_id=1, source_target_pairs={{0,4},{4,0},{1,5},{5,1},{2,6},{6,2},{3,7},{7,3}} | collective-permute-start | bytes 73736 | tf_op jit(solution)/shard_map/ppermute | solution.py:193
  115.5 397.6 %collective-permute-start.1 = (bf16[2048,1024]{1,0:T(8,128)(2,1)}, bf16[2048,1024]{1,0:T(8,128)(2,1)}, u32[]{:S(2)}, u32[]{:S(2)}) collective-permute-start(bf16[2048,1024]{1,0:T(8,128)(2,1)} %param.13), channel_id=1, source_target_pairs={{0,4},{4,0},{1,5},{5,1},{2,6},{6,2},{3,7},{7,3}} | collective-permute-start | bytes 12582920 | tf_op jit(solution)/shard_map/ppermute | solution.py:193
  115.9 268.2 %collective-permute-start.2 = (bf16[2048,1024]{1,0:T(8,128)(2,1)}, bf16[2048,1024]{1,0:T(8,128)(2,1)}, u32[]{:S(2)}, u32[]{:S(2)}) collective-permute-start(bf16[2048,1024]{1,0:T(8,128)(2,1)} %slice.50), channel_id=1, source_target_pairs={{0,4},{4,0},{1,5},{5,1},{2,6},{6,2},{3,7},{7,3}} | collective-permute-start | bytes 12582920 | tf_op jit(solution)/shard_map/ppermute | solution.py:193
  513.1 691.1 %reduce-scatter.5.cloned.1.call-start = ((), (), s32[]{:S(2)}) async-start(), calls=%async_computation.7 | async-start | bytes 41943040 | tf_op jit(solution)/shard_map/reduce_scatter | solution.py:241
  593.9 1.3 copy-start.13
  593.9 616.4 %reduce-scatter.3.cloned.1.call-start = ((), (), s32[]{:S(2)}) async-start(), calls=%async_computation.6 | async-start | bytes 31457280 | tf_op jit(solution)/shard_map/reduce_scatter | solution.py:252
  594.0 180.1 %collective-permute-start = (bf16[4096,1024]{1,0:T(8,128)(2,1)}, bf16[4096,1024]{1,0:T(8,128)(2,1)}, u32[]{:S(2)}, u32[]{:S(2)}) collective-permute-start(bf16[4096,1024]{1,0:T(8,128)(2,1)} %yl_ref.3), channel_id=1, source_target_pairs={{0,4},{4,0},{1,5},{5,1},{2,6},{6,2},{3,7},{7,3}} | collective-permute-start | bytes 25165832 | tf_op jit(solution)/shard_map/ppermute | solution.py:193
  919.3 5.9 copy-start.1
  919.3 5.9 copy-start.2
  919.3 5.9 copy-start
  927.7 27.9 %copy-start.4 = (f32[16,4096]{1,0:T(8,128)S(1)}, f32[16,4096]{1,0:T(8,128)}, u32[]{:S(2)}) copy-start(f32[16,4096]{1,0:T(8,128)} %get-tuple-element.88) | copy-start | bytes 786436
  1000.4 83.0 %copy-start.6 = (f32[4096]{0:T(1024)S(1)}, f32[4096]{0:T(1024)}, u32[]{:S(2)}) copy-start(f32[4096]{0:T(1024)} %get-tuple-element.94) | copy-start | bytes 49156
  1000.4 83.0 %copy-start.7 = (f32[4096]{0:T(1024)S(1)}, f32[4096]{0:T(1024)}, u32[]{:S(2)}) copy-start(f32[4096]{0:T(1024)} %get-tuple-element.95) | copy-start | bytes 49156
  1000.4 83.0 %copy-start.10 = (f32[1024]{0:T(1024)S(1)}, f32[1024]{0:T(1024)}, u32[]{:S(2)}) copy-start(f32[1024]{0:T(1024)} %param.9) | copy-start | bytes 12292
  1083.5 48.4 %copy-start.5 = (f32[4096]{0:T(1024)S(1)}, f32[4096]{0:T(1024)}, u32[]{:S(2)}) copy-start(f32[4096]{0:T(1024)} %reduce_sum.56) | copy-start | bytes 49156
  1083.5 48.3 %copy-start.8 = (f32[1024]{0:T(1024)S(1)}, f32[1024]{0:T(1024)}, u32[]{:S(2)}) copy-start(f32[1024]{0:T(1024)} %convert_reduce_fusion) | copy-start | bytes 12292
  1131.8 16.7 %collective-permute-start.11 = (f32[7168]{0:T(1024)S(1)}, f32[7168]{0:T(1024)S(1)}, u32[]{:S(2)}, u32[]{:S(2)}) collective-permute-start(f32[7168]{0:T(1024)S(1)} %pad_maximum_fusion.2), channel_id=1, source_target_pairs={{0,1},{1,0},{2,3},{3,2},{4,5},{5,4},{6,7},{7,6}} | collective-permute-start | bytes 86024 | tf_op jit(solution)/shard_map/ppermute | solution.py:280
  1141.3 11.2 collective-permute-start.9
  1144.7 27.4 %collective-permute-start.8 = (f32[512,1024]{1,0:T(8,128)}, f32[512,1024]{1,0:T(8,128)}, u32[]{:S(2)}, u32[]{:S(2)}) collective-permute-start(f32[512,1024]{1,0:T(8,128)} %copy.35), channel_id=1, source_target_pairs={{0,1},{1,0},{2,3},{3,2},{4,5},{5,4},{6,7},{7,6}} | collective-permute-start | bytes 6291464 | tf_op jit(solution)/shard_map/ppermute | solution.py:263
  1148.5 3.9 collective-permute-start.7
  1148.6 22.3 %collective-permute-start.12 = (f32[7168]{0:T(1024)S(1)}, f32[7168]{0:T(1024)S(1)}, u32[]{:S(2)}, u32[]{:S(2)}) collective-permute-start(f32[7168]{0:T(1024)S(1)} %fusion.21), channel_id=1, source_target_pairs={{0,2},{2,0},{1,3},{3,1},{4,6},{6,4},{5,7},{7,5}} | collective-permute-start | bytes 86024 | tf_op jit(solution)/shard_map/ppermute | solution.py:281
  1155.2 46.9 %collective-permute-start.10 = (f32[512,1024]{1,0:T(8,128)S(1)}, f32[512,1024]{1,0:T(8,128)S(1)}, u32[]{:S(2)}, u32[]{:S(2)}) collective-permute-start(f32[512,1024]{1,0:T(8,128)S(1)} %add.89), channel_id=1, source_target_pairs={{0,2},{2,0},{1,3},{3,1},{4,6},{6,4},{5,7},{7,5}} | collective-permute-start | bytes 6291464 | tf_op jit(solution)/shard_map/ppermute | solution.py:264
Sparse Core Ops, SparseCore 0:
  9.5 105.9 all-gather.4
  117.0 103.1 all-gather.6
  221.7 103.1 all-gather.8
  513.3 103.8 all-gather.10
  619.6 226.7 reduce-scatter.4
  919.5 176.8 reduce-scatter.2
